TPU v7x, 8 devices: a whole 2x2x1 slice. The times are simulated.
8 devices in a mesh: dp: 1 (over z), tp: 2 (over y), cp: 4 (over x, core).
Axes of the slice: x: 2, y: 2, z: 1, core: 2. Of those that a mesh axis runs over, the one named last changes fastest.
Arguments:
- hidden: bfloat16 [4096, 3072], P(('dp', 'cp'))
- positions: int32 [4096], P(('dp', 'cp'))
- ln_gain: bfloat16 [3072], replicated
- w_q: bfloat16 [3072, 3072], P(None, 'tp')
- w_k: bfloat16 [3072, 1024], P(None, 'tp')
- w_v: bfloat16 [3072, 1024], P(None, 'tp')
- w_o: bfloat16 [3072, 3072], P('tp')
- w_gate: bfloat16 [3072, 8192], P(None, 'tp')
- w_up: bfloat16 [3072, 8192], P(None, 'tp')
- w_down: bfloat16 [8192, 3072], P('tp')
Outputs:
- output 1: bfloat16 [4096, 3072], P(('dp', 'cp'))
- output 2: bfloat16 [4096, 8, 128], P(('dp', 'cp'), 'tp')
- output 3: bfloat16 [4096, 8, 128], P(('dp', 'cp'), 'tp')
All inputs are finite; a program needn't handle non-finite values.
Results may differ from a plain program's by a relative error of at most 0.0123478.
Values are sent between devices in bfloat16 or wider.
A program may use at most 1 GiB of HBM per device.

v0:
```python
import functools

import jax
import jax.numpy as jnp
from jax import lax
from jax.experimental import pallas as pl
from jax.experimental.pallas import tpu as pltpu
from jax.sharding import PartitionSpec as P


HEAD_DIM = 128
ROPE_BASE = 4000000
LN_EPS = 1e-5
CHUNK = 512
LOG2E = 1.4426950408889634
BF16 = jnp.bfloat16
F32 = jnp.float32


def cost(flops, bytes_accessed, transcendentals=0):
    return pl.CostEstimate(flops=int(flops), bytes_accessed=int(bytes_accessed), transcendentals=int(transcendentals))


def rotary_tables(positions):
    lane = jnp.arange(HEAD_DIM)
    exponent = ((lane // 2) * 2).astype(F32) / HEAD_DIM
    inv_freq = 1.0 / (ROPE_BASE ** exponent)
    angles = positions.astype(F32)[:, None] * inv_freq[None, :]
    sign = jnp.where(lane % 2 == 0, -1.0, 1.0).astype(F32)
    return jnp.cos(angles), jnp.sin(angles) * sign[None, :]


def rotate_head(head, cosine, sine):
    even = lax.broadcasted_iota(jnp.int32, head.shape, 1) % 2 == 0
    other = jnp.where(even, pltpu.roll(head, HEAD_DIM - 1, 1), pltpu.roll(head, 1, 1))
    return (head * cosine + other * sine).astype(BF16)


def norm_kv_kernel(x_ref, gain_ref, wk_ref, wv_ref, cos_ref, sin_ref, h_ref, kv_ref, k_ref, v_ref):
    x = x_ref[...].astype(F32)
    width = x.shape[1]
    mean = jnp.sum(x, axis=1, keepdims=True) * (1.0 / width)
    centered = x - mean
    var = jnp.sum(centered * centered, axis=1, keepdims=True) * (1.0 / width)
    h = (centered * lax.rsqrt(var + LN_EPS) * gain_ref[...].astype(F32)[None, :]).astype(BF16)
    h_ref[...] = h
    k = jnp.dot(h_ref[...], wk_ref[...], preferred_element_type=F32).astype(BF16)
    v = jnp.dot(h_ref[...], wv_ref[...], preferred_element_type=F32).astype(BF16)
    v_ref[...] = v
    cosine, sine = cos_ref[...], sin_ref[...]
    for head in range(k.shape[1] // HEAD_DIM):
        cols = slice(head * HEAD_DIM, (head + 1) * HEAD_DIM)
        rotated = rotate_head(k[:, cols].astype(F32), cosine, sine)
        k_ref[:, cols] = rotated
        kv_ref[head, 0] = rotated
        for start in range(0, k.shape[0], HEAD_DIM):
            kv_ref[head, 1, start:start + HEAD_DIM, :] = v[start:start + HEAD_DIM, cols].T


def norm_kv(x, gain, wk, wv, cosine, sine):
    rows, width = x.shape
    kv = wk.shape[1]
    groups = kv // HEAD_DIM
    tile = 256
    return pl.pallas_call(
        norm_kv_kernel,
        grid=(rows // tile,),
        in_specs=[
            pl.BlockSpec((tile, width), lambda i: (i, 0)),
            pl.BlockSpec((width,), lambda i: (0,)),
            pl.BlockSpec((width, kv), lambda i: (0, 0)),
            pl.BlockSpec((width, kv), lambda i: (0, 0)),
            pl.BlockSpec((tile, HEAD_DIM), lambda i: (i, 0)),
            pl.BlockSpec((tile, HEAD_DIM), lambda i: (i, 0)),
        ],
        out_specs=[
            pl.BlockSpec((tile, width), lambda i: (i, 0)),
            pl.BlockSpec((groups, 2, tile, HEAD_DIM), lambda i: (0, 0, i, 0)),
            pl.BlockSpec((tile, kv), lambda i: (i, 0)),
            pl.BlockSpec((tile, kv), lambda i: (i, 0)),
        ],
        out_shape=[
            jax.ShapeDtypeStruct((rows, width), BF16),
            jax.ShapeDtypeStruct((groups, 2, rows, HEAD_DIM), BF16),
            jax.ShapeDtypeStruct((rows, kv), BF16),
            jax.ShapeDtypeStruct((rows, kv), BF16),
        ],
        cost_estimate=cost(4 * rows * width * kv, 4 * rows * width + 4 * width * kv),
        name='norm_kv',
    )(x, gain, wk, wv, cosine, sine)


def q_kernel(h_ref, w_ref, cos_ref, sin_ref, q_ref):
    q = jnp.dot(h_ref[...], w_ref[...], preferred_element_type=F32).astype(BF16)
    cosine, sine = cos_ref[...], sin_ref[...]
    for head in range(q.shape[1] // HEAD_DIM):
        cols = slice(head * HEAD_DIM, (head + 1) * HEAD_DIM)
        q_ref[:, cols] = rotate_head(q[:, cols].astype(F32), cosine, sine)


def q_proj(h, wq, cosine, sine):
    rows, width = h.shape
    cols = wq.shape[1]
    tile = 512
    return pl.pallas_call(
        q_kernel,
        grid=(cols // tile,),
        in_specs=[
            pl.BlockSpec((rows, width), lambda i: (0, 0)),
            pl.BlockSpec((width, tile), lambda i: (0, i)),
            pl.BlockSpec((rows, HEAD_DIM), lambda i: (0, 0)),
            pl.BlockSpec((rows, HEAD_DIM), lambda i: (0, 0)),
        ],
        out_specs=pl.BlockSpec((rows, tile), lambda i: (0, i)),
        out_shape=jax.ShapeDtypeStruct((rows, cols), BF16),
        cost_estimate=cost(2 * rows * width * cols, 2 * rows * width + 2 * width * cols),
        name='q_proj',
    )(h, wq, cosine, sine)


def attend_kernel(base, tile, group, blocks, flags_ref, q_ref, *refs):
    sources = refs[:1 + sum(blocks)]
    o_ref, m_ref, l_ref, acc_ref, s0_ref, s1_ref = refs[1 + sum(blocks):]
    scale2 = (HEAD_DIM ** -0.5) * LOG2E
    step = pl.program_id(1)

    def scores(kv, keys, j, buffer, masked):
        q = q_ref[:, j * HEAD_DIM:(j + 1) * HEAD_DIM]
        top = None
        for start in range(0, keys, CHUNK):
            size = min(CHUNK, keys - start)
            s = lax.dot_general(kv[0, start:start + size, :], q, (((1,), (1,)), ((), ())), preferred_element_type=F32)
            if masked and start + size > keys - tile:
                key = lax.broadcasted_iota(jnp.int32, s.shape, 0) + start
                query = lax.broadcasted_iota(jnp.int32, s.shape, 1) + (keys - tile)
                s = jnp.where(key <= query, s, -jnp.inf)
            buffer[start:start + size, :] = s
            part = jnp.max(s.reshape(size // 8, 8, tile), axis=0)
            top = part if top is None else jnp.maximum(top, part)
        return top

    def block(full, keys, first, masked):
        items = [(kv, j) for kv in full for j in range(group)]
        buffers = (s0_ref, s1_ref)
        top8 = scores(items[0][0], keys, items[0][1], buffers[0], masked)
        for n, (kv, j) in enumerate(items):
            top = jnp.max(top8, axis=0, keepdims=True)
            if not first:
                old = m_ref[j]
                top = jnp.maximum(top, old)
            if n + 1 < len(items):
                top8 = scores(items[n + 1][0], keys, items[n + 1][1], buffers[(n + 1) % 2], masked)
            total = part = None
            for start in range(0, keys, CHUNK):
                size = min(CHUNK, keys - start)
                e = jnp.exp2((buffers[n % 2][start:start + size, :] - top) * scale2)
                e8 = jnp.sum(e.reshape(size // 8, 8, tile), axis=0)
                vt = jnp.concatenate([kv[1, at:at + HEAD_DIM, :] for at in range(start, start + size, HEAD_DIM)], axis=1)
                product = lax.dot_general(vt, e.astype(BF16), (((1,), (0,)), ((), ())), preferred_element_type=F32)
                total = e8 if total is None else total + e8
                part = product if part is None else part + product
            total = jnp.sum(total, axis=0, keepdims=True)
            if not first:
                factor = jnp.exp2((old - top) * scale2)
                total = total + l_ref[j] * factor
                part = part + acc_ref[j] * factor
            m_ref[j] = top
            l_ref[j] = total
            acc_ref[j] = part

    for n in range(pl.num_programs(1)):

        @pl.when(step == n)
        def _():
            block(sources[:1], base + (n + 1) * tile, True, True)

    start = 1
    for flag, many in enumerate(blocks):
        full = sources[start:start + many]
        start += many

        @pl.when(flags_ref[flag] > 0)
        def _():
            block(full, full[0].shape[1], False, False)

    for j in range(group):
        out = acc_ref[j] / l_ref[j]
        o_ref[:, j * HEAD_DIM:(j + 1) * HEAD_DIM] = out.T.astype(BF16)


def attend(flags, q, base, count, groups, sources, blocks):
    keys = sources[0].shape[2]
    width = q.shape[1] // groups
    group = width // HEAD_DIM
    tile = 256
    first = base // tile

    kv_spec = pl.BlockSpec((None, 2, keys, HEAD_DIM), lambda g, i, f: (g, 0, 0, 0))
    grid_spec = pltpu.PrefetchScalarGridSpec(
        num_scalar_prefetch=1,
        grid=(groups, count // tile),
        in_specs=[pl.BlockSpec((tile, width), lambda g, i, f: (first + i, g))] + [kv_spec] * len(sources),
        out_specs=pl.BlockSpec((tile, width), lambda g, i, f: (i, g)),
        scratch_shapes=[
            pltpu.VMEM((group, 1, tile), F32),
            pltpu.VMEM((group, 1, tile), F32),
            pltpu.VMEM((group, HEAD_DIM, tile), F32),
            pltpu.VMEM((keys, tile), F32),
            pltpu.VMEM((keys, tile), F32),
        ],
    )
    return pl.pallas_call(
        functools.partial(attend_kernel, base, tile, group, blocks),
        grid_spec=grid_spec,
        out_shape=jax.ShapeDtypeStruct((count, q.shape[1]), BF16),
        cost_estimate=cost(10 * count * keys * q.shape[1], 4 * len(sources) * keys * groups * HEAD_DIM, 3 * count * keys * groups * group),
        name='attend',
    )(flags, q, *sources)


def gate_up_kernel(h_ref, wg_ref, wu_ref, a_ref):
    gate = jnp.dot(h_ref[...], wg_ref[...], preferred_element_type=F32).astype(BF16).astype(F32)
    up = jnp.dot(h_ref[...], wu_ref[...], preferred_element_type=F32).astype(BF16).astype(F32)
    a_ref[...] = (gate * jax.nn.sigmoid(gate) * up).astype(BF16)


def gate_up(h, wg, wu, first, rows):
    width, cols = wg.shape
    tile = 512
    index = first // rows
    weight_spec = pl.BlockSpec((width, tile), lambda i: (0, i))
    return pl.pallas_call(
        gate_up_kernel,
        grid=(cols // tile,),
        in_specs=[pl.BlockSpec((rows, width), lambda i: (index, 0)), weight_spec, weight_spec],
        out_specs=pl.BlockSpec((rows, tile), lambda i: (0, i)),
        out_shape=jax.ShapeDtypeStruct((rows, cols), BF16),
        cost_estimate=cost(4 * rows * width * cols, 2 * rows * (width + cols) + 4 * width * cols),
        name='gate_up',
    )(h, wg, wu)


def down_kernel(a_ref, o_ref, wd_ref, wo_ref, out_ref):
    total = jnp.dot(a_ref[...], wd_ref[...], preferred_element_type=F32)
    total += jnp.dot(o_ref[...], wo_ref[...], preferred_element_type=F32)
    out_ref[...] = total.astype(BF16)


def down(a, o, wd, wo, a_row, o_row, rows, col, cols):
    tile = 512
    start = col // tile
    return pl.pallas_call(
        down_kernel,
        grid=(cols // tile,),
        in_specs=[
            pl.BlockSpec((rows, a.shape[1]), lambda i: (a_row // rows, 0)),
            pl.BlockSpec((rows, o.shape[1]), lambda i: (o_row // rows, 0)),
            pl.BlockSpec((wd.shape[0], tile), lambda i: (0, start + i)),
            pl.BlockSpec((wo.shape[0], tile), lambda i: (0, start + i)),
        ],
        out_specs=pl.BlockSpec((rows, tile), lambda i: (0, i)),
        out_shape=jax.ShapeDtypeStruct((rows, cols), BF16),
        cost_estimate=cost(2 * rows * (wd.shape[0] + wo.shape[0]) * cols, 2 * cols * (wd.shape[0] + wo.shape[0])),
        name='down',
    )(a, o, wd, wo)


def add_kernel(x_ref, mine_ref, other_ref, *refs):
    total = mine_ref[...].astype(F32) + other_ref[...].astype(F32)
    refs[-1][...] = (x_ref[...].astype(F32) + total).astype(BF16)


def add_chunk(x, mine, other, out, first, col):
    rows, cols = mine.shape
    tile = min(256, rows)
    index, start = first // tile, col // cols
    place = pl.BlockSpec((tile, cols), lambda i: (index + i, start))
    chunk = pl.BlockSpec((tile, cols), lambda i: (i, 0))
    args, specs, alias = [x, mine, other], [place, chunk, chunk], {}
    if out is not None:
        args, specs, alias = args + [out], specs + [pl.BlockSpec(memory_space=pl.ANY)], {3: 0}
    return pl.pallas_call(
        add_kernel,
        grid=(rows // tile,),
        in_specs=specs,
        out_specs=place,
        out_shape=jax.ShapeDtypeStruct(x.shape, BF16),
        input_output_aliases=alias,
        cost_estimate=cost(3 * rows * cols, 8 * rows * cols),
        name='add',
    )(*args)


SCHEDULE = (
    ('mlp', 0, 512),
    ('own', 0, 256),
    ('down', 0, 256, 0, 3072),
    ('own', 256, 256),
    ('down', 256, 256, 0, 3072),
    ('mlp', 512, 512),
    ('own', 512, 256),
    ('down', 512, 256, 0, 3072),
    ('own', 768, 256),
    ('down', 768, 256, 0, 1536),
    ('down', 768, 256, 1536, 1536),
)


def solution(mesh):
    if mesh.shape['cp'] != 4 or mesh.shape['tp'] != 2:
        raise ValueError('mesh')

    def local_layer(hidden, positions, ln_gain, w_q, w_k, w_v, w_o, w_gate, w_up, w_down):
        me = lax.axis_index('cp')
        cosine, sine = rotary_tables(positions)
        normed, kv_own, k_own, v_own = norm_kv(hidden, ln_gain, w_k, w_v, cosine, sine)
        groups = kv_own.shape[0]
        send = functools.partial(lax.ppermute, axis_name='cp')
        kv_b = send(kv_own, perm=[(0, 2), (1, 3)])
        kv_a = send(kv_own, perm=[(0, 1), (2, 3)])
        kv_c = send(kv_b, perm=[(2, 3), (3, 2)])
        flags = jnp.stack([me % 2, me // 2]).astype(jnp.int32)
        q_rot = q_proj(normed, w_q, cosine, sine)
        last = q_rot
        acts, attns, pieces = [], [], []
        for kind, first, rows, *place in SCHEDULE:
            if kind == 'mlp':
                normed, last = lax.optimization_barrier((normed, last))
                last = gate_up(normed, w_gate, w_up, first, rows)
                acts.append((first, last))
            if kind == 'own':
                q_rot, last = lax.optimization_barrier((q_rot, last))
                sources = (kv_own, kv_a, kv_b, kv_c)
                last = attend(flags, q_rot, first, rows, groups, sources, (1, 2))
                attns.append((first, last))
            if kind == 'down':
                col, cols = place
                (a_first, act), (o_first, attn) = [[pair for pair in pairs if pair[0] <= first][-1] for pairs in (acts, attns)]
                act, last = lax.optimization_barrier((act, last))
                last = down(act, attn, w_down, w_o, first - a_first, first - o_first, rows, col, cols)
                other = lax.ppermute(last, 'tp', [(0, 1), (1, 0)])
                pieces.append((last, other, first, col))
        k_own, v_own, last = lax.optimization_barrier((k_own, v_own, last))
        cache_shape = (k_own.shape[0], groups, HEAD_DIM)
        k_cache, v_cache = k_own.reshape(cache_shape), v_own.reshape(cache_shape)
        hidden_out = None
        for part, other, first, col in pieces:
            hidden_out = add_chunk(hidden, part, other, hidden_out, first, col)
        return hidden_out, k_cache, v_cache

    row_spec = P(('dp', 'cp'), None)
    col_spec = P(None, 'tp')
    cache_spec = P(('dp', 'cp'), 'tp', None)
    in_specs = (row_spec, P(('dp', 'cp')), P(None), col_spec, col_spec, col_spec, P('tp', None), col_spec, col_spec, P('tp', None))
    return jax.shard_map(local_layer, mesh=mesh, in_specs=in_specs, out_specs=(row_spec, cache_spec, cache_spec), check_vma=False)
```

profile of v0, /device:TPU:3, one launch (start us, length us, event | category | flops | bytes accessed | tf_op | source)
XLA Modules:
  0.0 371.1 jit_solution(11185033178687046026)
XLA Ops:
  0.6 0.7 convert_element_type.10
  1.3 3.0 fusion
  4.4 15.6 %norm_kv.1 = (bf16[1024,3072]{1,0:T(8,128)(2,1)}, bf16[4,2,1024,128]{3,2,1,0:T(8,128)(2,1)}, bf16[1024,512]{1,0:T(8,128)(2,1)}, bf16[1024,512]{1,0:T(8,128)(2,1)}) custom-call(bf16[1024,3072]{1,0:T(8,128)(2,1)} %x_ref.11, bf16[3072]{0:T(1024)(128)(2,1)} %gain_ref.1, bf16[3072,512]{1,0:T(8,128)(2,1)} %wk_ref.1, bf16[3072,512]{1,0:T(8,128)(2,1)} %wv_ref.1, ...), custom_call_target="tpu_custom_call" | custom-call | flops 6442450944 | bytes 18874368 | tf_op jit(solution)/shard_map/norm_kv/pallas_call | solution.py:65
  19.9 1.3 collective-permute-start.1
  21.2 1.3 collective-permute-start
  22.5 16.6 %q_proj.1.q_ref = bf16[1024,1536]{1,0:T(8,128)(2,1)} custom-call(bf16[1024,3072]{1,0:T(8,128)(2,1)} %get-tuple-element.27.h_ref, bf16[3072,1536]{1,0:T(8,128)(2,1)} %w_ref.1, f32[1024,128]{1,0:T(8,128)} %get-tuple-element.38.cos_ref, f32[1024,128]{1,0:T(8,128)} %get-tuple-element.37.sin_ref), custom_call_target="tpu_custom_call" | custom-call | flops 9663676416 | bytes 15728640 | tf_op jit(solution)/shard_map/q_proj/pallas_call | solution.py:105
  39.2 29.4 %collective-permute-done.1.refs_2_ = bf16[4,2,1024,128]{3,2,1,0:T(8,128)(2,1)S(1)} collective-permute-done((bf16[4,2,1024,128]{3,2,1,0:T(8,128)(2,1)}, bf16[4,2,1024,128]{3,2,1,0:T(8,128)(2,1)S(1)}, u32[]{:S(2)}, u32[]{:S(2)}) %collective-permute-start.1) | collective-permute-done | bytes 2097184 | tf_op jit(solution)/shard_map/ppermute | solution.py:319
  68.5 0.0 copy-start.2
  68.5 3.6 collective-permute-start.2
  72.2 32.4 %gate_up.2.a_ref = bf16[512,4096]{1,0:T(8,128)(2,1)} custom-call(bf16[1024,3072]{1,0:T(8,128)(2,1)} %get-tuple-element.27.h_ref, bf16[3072,4096]{1,0:T(8,128)(2,1)} %wg_ref.3, bf16[3072,4096]{1,0:T(8,128)(2,1)} %wu_ref.3), custom_call_target="tpu_custom_call" | custom-call | flops 25769803776 | bytes 57671680 | tf_op jit(solution)/shard_map/gate_up/pallas_call | solution.py:232
  104.6 0.0 copy-done.2
  104.6 0.6 pad_add_fusion.flags_ref
  105.2 0.0 collective-permute-done.refs_1_
  105.2 0.0 collective-permute-done.2.refs_3_
  105.2 17.6 %attend.4.o_ref = bf16[256,1536]{1,0:T(8,128)(2,1)} custom-call(s32[2]{0:T(128)} %pad_add_fusion.flags_ref, bf16[1024,1536]{1,0:T(8,128)(2,1)} %q_proj.1.q_ref, bf16[4,2,1024,128]{3,2,1,0:T(8,128)(2,1)} %get-tuple-element.23.refs_0_, bf16[4,2,1024,128]{3,2,1,0:T(8,128)(2,1)} %collective-permute-done.refs_1_, bf16[4,2,1024,128]{3,2,1,0:T(8,128)(2,1)} %copy-done.2, ...), custom_call_target="tpu_custom_call" | custom-call | flops 4026531840 | bytes 8388608 | tf_op jit(solution)/shard_map/attend/pallas_call | solution.py:212
  122.8 17.0 %down.5.mine_ref = bf16[256,3072]{1,0:T(8,128)(2,1)} custom-call(bf16[512,4096]{1,0:T(8,128)(2,1)} %gate_up.2.a_ref, bf16[256,1536]{1,0:T(8,128)(2,1)} %attend.4.o_ref, bf16[4096,3072]{1,0:T(8,128)(2,1)} %wd_ref.9, bf16[1536,3072]{1,0:T(8,128)(2,1)} %wo_ref.9), custom_call_target="tpu_custom_call" | custom-call | flops 8858370048 | bytes 34603008 | tf_op jit(solution)/shard_map/down/pallas_call | solution.py:252
  139.8 18.4 %attend.5.o_ref = bf16[256,1536]{1,0:T(8,128)(2,1)} custom-call(s32[2]{0:T(128)} %pad_add_fusion.flags_ref, bf16[1024,1536]{1,0:T(8,128)(2,1)} %q_proj.1.q_ref, bf16[4,2,1024,128]{3,2,1,0:T(8,128)(2,1)} %get-tuple-element.23.refs_0_, bf16[4,2,1024,128]{3,2,1,0:T(8,128)(2,1)} %collective-permute-done.refs_1_, bf16[4,2,1024,128]{3,2,1,0:T(8,128)(2,1)} %copy-done.2, ...), custom_call_target="tpu_custom_call" | custom-call | flops 4026531840 | bytes 8388608 | tf_op jit(solution)/shard_map/attend/pallas_call | solution.py:212
  158.3 16.9 %down.6.mine_ref = bf16[256,3072]{1,0:T(8,128)(2,1)} custom-call(bf16[512,4096]{1,0:T(8,128)(2,1)} %gate_up.2.a_ref, bf16[256,1536]{1,0:T(8,128)(2,1)} %attend.5.o_ref, bf16[4096,3072]{1,0:T(8,128)(2,1)} %wd_ref.9, bf16[1536,3072]{1,0:T(8,128)(2,1)} %wo_ref.9), custom_call_target="tpu_custom_call" | custom-call | flops 8858370048 | bytes 34603008 | tf_op jit(solution)/shard_map/down/pallas_call | solution.py:252
  175.2 32.4 %gate_up.3.a_ref = bf16[512,4096]{1,0:T(8,128)(2,1)} custom-call(bf16[1024,3072]{1,0:T(8,128)(2,1)} %get-tuple-element.27.h_ref, bf16[3072,4096]{1,0:T(8,128)(2,1)} %wg_ref.3, bf16[3072,4096]{1,0:T(8,128)(2,1)} %wu_ref.3), custom_call_target="tpu_custom_call" | custom-call | flops 25769803776 | bytes 57671680 | tf_op jit(solution)/shard_map/gate_up/pallas_call | solution.py:232
  207.6 19.5 %attend.6.o_ref = bf16[256,1536]{1,0:T(8,128)(2,1)} custom-call(s32[2]{0:T(128)} %pad_add_fusion.flags_ref, bf16[1024,1536]{1,0:T(8,128)(2,1)} %q_proj.1.q_ref, bf16[4,2,1024,128]{3,2,1,0:T(8,128)(2,1)} %get-tuple-element.23.refs_0_, bf16[4,2,1024,128]{3,2,1,0:T(8,128)(2,1)} %collective-permute-done.refs_1_, bf16[4,2,1024,128]{3,2,1,0:T(8,128)(2,1)} %copy-done.2, ...), custom_call_target="tpu_custom_call" | custom-call | flops 4026531840 | bytes 8388608 | tf_op jit(solution)/shard_map/attend/pallas_call | solution.py:212
  227.1 0.0 copy-start
  227.1 0.0 copy-start.1
  227.1 17.2 %down.7.mine_ref = bf16[256,3072]{1,0:T(8,128)(2,1)} custom-call(bf16[512,4096]{1,0:T(8,128)(2,1)} %gate_up.3.a_ref, bf16[256,1536]{1,0:T(8,128)(2,1)} %attend.6.o_ref, bf16[4096,3072]{1,0:T(8,128)(2,1)} %wd_ref.9, bf16[1536,3072]{1,0:T(8,128)(2,1)} %wo_ref.9), custom_call_target="tpu_custom_call" | custom-call | flops 8858370048 | bytes 34603008 | tf_op jit(solution)/shard_map/down/pallas_call | solution.py:252
  244.3 1.2 collective-permute-start.5
  245.5 0.0 copy-done
  245.5 0.2 collective-permute-start.6
  245.7 0.0 copy-done.1
  245.7 1.2 collective-permute-start.7
  247.0 20.3 %attend.7.o_ref = bf16[256,1536]{1,0:T(8,128)(2,1)} custom-call(s32[2]{0:T(128)} %pad_add_fusion.flags_ref, bf16[1024,1536]{1,0:T(8,128)(2,1)} %q_proj.1.q_ref, bf16[4,2,1024,128]{3,2,1,0:T(8,128)(2,1)} %get-tuple-element.23.refs_0_, bf16[4,2,1024,128]{3,2,1,0:T(8,128)(2,1)} %collective-permute-done.refs_1_, bf16[4,2,1024,128]{3,2,1,0:T(8,128)(2,1)} %copy-done.2, ...), custom_call_target="tpu_custom_call" | custom-call | flops 4026531840 | bytes 8388608 | tf_op jit(solution)/shard_map/attend/pallas_call | solution.py:212
  267.2 10.4 %down.8.mine_ref = bf16[256,1536]{1,0:T(8,128)(2,1)} custom-call(bf16[512,4096]{1,0:T(8,128)(2,1)} %gate_up.3.a_ref, bf16[256,1536]{1,0:T(8,128)(2,1)} %attend.7.o_ref, bf16[4096,3072]{1,0:T(8,128)(2,1)} %wd_ref.9, bf16[1536,3072]{1,0:T(8,128)(2,1)} %wo_ref.9), custom_call_target="tpu_custom_call" | custom-call | flops 4429185024 | bytes 17301504 | tf_op jit(solution)/shard_map/down/pallas_call | solution.py:252
  277.6 0.2 collective-permute-start.4
  277.9 10.4 %down.9.mine_ref = bf16[256,1536]{1,0:T(8,128)(2,1)} custom-call(bf16[512,4096]{1,0:T(8,128)(2,1)} %gate_up.3.a_ref, bf16[256,1536]{1,0:T(8,128)(2,1)} %attend.7.o_ref, bf16[4096,3072]{1,0:T(8,128)(2,1)} %wd_ref.9, bf16[1536,3072]{1,0:T(8,128)(2,1)} %wo_ref.9), custom_call_target="tpu_custom_call" | custom-call | flops 4429185024 | bytes 17301504 | tf_op jit(solution)/shard_map/down/pallas_call | solution.py:252
  288.3 1.2 collective-permute-start.3
  289.5 2.1 reshape.42
  291.6 2.1 reshape.43
  293.7 54.6 %collective-permute-done.7.other_ref = bf16[256,3072]{1,0:T(8,128)(2,1)} collective-permute-done((bf16[256,3072]{1,0:T(8,128)(2,1)S(1)}, bf16[256,3072]{1,0:T(8,128)(2,1)}, u32[]{:S(2)}, u32[]{:S(2)}) %collective-permute-start.7) | collective-permute-done | bytes 1572896 | tf_op jit(solution)/shard_map/ppermute | solution.py:341
  348.4 4.1 %add.32.refs_0_ = bf16[1024,3072]{1,0:T(8,128)(2,1)} custom-call(bf16[1024,3072]{1,0:T(8,128)(2,1)} %x_ref.11, bf16[256,3072]{1,0:T(8,128)(2,1)} %down.5.mine_ref, bf16[256,3072]{1,0:T(8,128)(2,1)} %collective-permute-done.7.other_ref), custom_call_target="tpu_custom_call" | custom-call | flops 2359296 | bytes 6291456 | tf_op jit(solution)/shard_map/add/pallas_call | solution.py:282
  352.4 0.0 collective-permute-done.6.other_ref
  352.4 4.1 %add.33.refs_0_ = bf16[1024,3072]{1,0:T(8,128)(2,1)} custom-call(bf16[1024,3072]{1,0:T(8,128)(2,1)} %x_ref.11, bf16[256,3072]{1,0:T(8,128)(2,1)} %down.6.mine_ref, bf16[256,3072]{1,0:T(8,128)(2,1)} %collective-permute-done.6.other_ref, bf16[1024,3072]{1,0:T(8,128)(2,1)} %add.32.refs_0_), custom_call_target="tpu_custom_call", output_to_operand_aliasing={{}: (3, {})} | custom-call | flops 2359296 | bytes 6291456 | tf_op jit(solution)/shard_map/add/pallas_call | solution.py:282
  356.5 0.0 collective-permute-done.5.other_ref
  356.5 4.1 %add.34.refs_0_ = bf16[1024,3072]{1,0:T(8,128)(2,1)} custom-call(bf16[1024,3072]{1,0:T(8,128)(2,1)} %x_ref.11, bf16[256,3072]{1,0:T(8,128)(2,1)} %down.7.mine_ref, bf16[256,3072]{1,0:T(8,128)(2,1)} %collective-permute-done.5.other_ref, bf16[1024,3072]{1,0:T(8,128)(2,1)} %add.33.refs_0_), custom_call_target="tpu_custom_call", output_to_operand_aliasing={{}: (3, {})} | custom-call | flops 2359296 | bytes 6291456 | tf_op jit(solution)/shard_map/add/pallas_call | solution.py:282
  360.6 0.0 collective-permute-done.4.other_ref
  360.6 2.8 add.35.refs_0_
  363.3 5.0 %collective-permute-done.3.other_ref = bf16[256,1536]{1,0:T(8,128)(2,1)} collective-permute-done((bf16[256,1536]{1,0:T(8,128)(2,1)}, bf16[256,1536]{1,0:T(8,128)(2,1)}, u32[]{:S(2)}, u32[]{:S(2)}) %collective-permute-start.3) | collective-permute-done | bytes 786464 | tf_op jit(solution)/shard_map/ppermute | solution.py:341
  368.4 2.8 add.36
  (1 shorter events, 0.0 us)
Async XLA Ops:
  19.9 48.6 %collective-permute-start.1 = (bf16[4,2,1024,128]{3,2,1,0:T(8,128)(2,1)}, bf16[4,2,1024,128]{3,2,1,0:T(8,128)(2,1)S(1)}, u32[]{:S(2)}, u32[]{:S(2)}) collective-permute-start(bf16[4,2,1024,128]{3,2,1,0:T(8,128)(2,1)} %get-tuple-element.23.refs_0_), channel_id=1, source_target_pairs={{0,2},{1,3},{4,6},{5,7}} | collective-permute-start | bytes 6291464 | tf_op jit(solution)/shard_map/ppermute | solution.py:319
  21.2 84.0 %collective-permute-start = (bf16[4,2,1024,128]{3,2,1,0:T(8,128)(2,1)}, bf16[4,2,1024,128]{3,2,1,0:T(8,128)(2,1)}, u32[]{:S(2)}, u32[]{:S(2)}) collective-permute-start(bf16[4,2,1024,128]{3,2,1,0:T(8,128)(2,1)} %get-tuple-element.23.refs_0_), channel_id=1, source_target_pairs={{0,1},{2,3},{4,5},{6,7}} | collective-permute-start | bytes 6291464 | tf_op jit(solution)/shard_map/ppermute | solution.py:320
  68.5 36.1 %copy-start.2 = (bf16[4,2,1024,128]{3,2,1,0:T(8,128)(2,1)}, bf16[4,2,1024,128]{3,2,1,0:T(8,128)(2,1)S(1)}, u32[]{:S(2)}) copy-start(bf16[4,2,1024,128]{3,2,1,0:T(8,128)(2,1)S(1)} %collective-permute-done.1.refs_2_) | copy-start | bytes 6291460
  68.5 36.7 %collective-permute-start.2 = (bf16[4,2,1024,128]{3,2,1,0:T(8,128)(2,1)S(1)}, bf16[4,2,1024,128]{3,2,1,0:T(8,128)(2,1)}, u32[]{:S(2)}, u32[]{:S(2)}) collective-permute-start(bf16[4,2,1024,128]{3,2,1,0:T(8,128)(2,1)S(1)} %collective-permute-done.1.refs_2_), channel_id=1, source_target_pairs={{2,3},{3,2},{6,7},{7,6}} | collective-permute-start | bytes 6291464 | tf_op jit(solution)/shard_map/ppermute | solution.py:321
  227.1 18.4 %copy-start = (bf16[256,3072]{1,0:T(8,128)(2,1)S(1)}, bf16[256,3072]{1,0:T(8,128)(2,1)}, u32[]{:S(2)}) copy-start(bf16[256,3072]{1,0:T(8,128)(2,1)} %down.6.mine_ref) | copy-start | bytes 4718596
  227.1 18.6 %copy-start.1 = (bf16[256,3072]{1,0:T(8,128)(2,1)S(1)}, bf16[256,3072]{1,0:T(8,128)(2,1)}, u32[]{:S(2)}) copy-start(bf16[256,3072]{1,0:T(8,128)(2,1)} %down.5.mine_ref) | copy-start | bytes 4718596
  244.3 112.3 %collective-permute-start.5 = (bf16[256,3072]{1,0:T(8,128)(2,1)}, bf16[256,3072]{1,0:T(8,128)(2,1)}, u32[]{:S(2)}, u32[]{:S(2)}) collective-permute-start(bf16[256,3072]{1,0:T(8,128)(2,1)} %down.7.mine_ref), channel_id=1, source_target_pairs={{0,4},{4,0},{1,5},{5,1},{2,6},{6,2},{3,7},{7,3}} | collective-permute-start | bytes 4718600 | tf_op jit(solution)/shard_map/ppermute | solution.py:341
  245.5 107.0 %collective-permute-start.6 = (bf16[256,3072]{1,0:T(8,128)(2,1)S(1)}, bf16[256,3072]{1,0:T(8,128)(2,1)}, u32[]{:S(2)}, u32[]{:S(2)}) collective-permute-start(bf16[256,3072]{1,0:T(8,128)(2,1)S(1)} %copy-done), channel_id=1, source_target_pairs={{0,4},{4,0},{1,5},{5,1},{2,6},{6,2},{3,7},{7,3}} | collective-permute-start | bytes 4718600 | tf_op jit(solution)/shard_map/ppermute | solution.py:341
  245.7 102.7 %collective-permute-start.7 = (bf16[256,3072]{1,0:T(8,128)(2,1)S(1)}, bf16[256,3072]{1,0:T(8,128)(2,1)}, u32[]{:S(2)}, u32[]{:S(2)}) collective-permute-start(bf16[256,3072]{1,0:T(8,128)(2,1)S(1)} %copy-done.1), channel_id=1, source_target_pairs={{0,4},{4,0},{1,5},{5,1},{2,6},{6,2},{3,7},{7,3}} | collective-permute-start | bytes 4718600 | tf_op jit(solution)/shard_map/ppermute | solution.py:341
  277.6 82.9 %collective-permute-start.4 = (bf16[256,1536]{1,0:T(8,128)(2,1)}, bf16[256,1536]{1,0:T(8,128)(2,1)}, u32[]{:S(2)}, u32[]{:S(2)}) collective-permute-start(bf16[256,1536]{1,0:T(8,128)(2,1)} %down.8.mine_ref), channel_id=1, source_target_pairs={{0,4},{4,0},{1,5},{5,1},{2,6},{6,2},{3,7},{7,3}} | collective-permute-start | bytes 2359304 | tf_op jit(solution)/shard_map/ppermute | solution.py:341
  288.3 80.1 %collective-permute-start.3 = (bf16[256,1536]{1,0:T(8,128)(2,1)}, bf16[256,1536]{1,0:T(8,128)(2,1)}, u32[]{:S(2)}, u32[]{:S(2)}) collective-permute-start(bf16[256,1536]{1,0:T(8,128)(2,1)} %down.9.mine_ref), channel_id=1, source_target_pairs={{0,4},{4,0},{1,5},{5,1},{2,6},{6,2},{3,7},{7,3}} | collective-permute-start | bytes 2359304 | tf_op jit(solution)/shard_map/ppermute | solution.py:341
where the time goes:
time: 372 us; the launch traced here: 371 us
  Pallas kernels  262 us (70%)
  waiting for transfers between devices  89 us (24%)
  starting transfers between devices  10.3 us (3%)
  other arithmetic  4.35 us (1%)
  local copies, waits for them, and re-layouts  4.28 us (1%)
    pallas_call x4, Pallas kernels, attend(): pl.pallas_call(functools.partial(attend_kernel, base, tile, group, blocks...  75.8 us
    pallas_call x5, Pallas kernels, down(): pl.pallas_call(down_kernel, grid=(cols // tile,), in_specs=[pl.BlockSpec(...  71.9 us
    pallas_call x2, Pallas kernels, gate_up(): pl.pallas_call(gate_up_kernel, grid=(cols // tile,), in_specs=[pl.BlockSp...  64.8 us
    ppermute x5, waiting for transfers between devices, local_layer(): other = lax.ppermute(last, 'tp', [(0, 1), (1, 0)])  59.7 us
    ppermute x1, waiting for transfers between devices, local_layer(): kv_b = send(kv_own, perm=[(0, 2), (1, 3)])  29.4 us
    pallas_call x5, Pallas kernels, add_chunk(): pl.pallas_call(add_kernel, grid=(rows // tile,), in_specs=specs, out_spec...  17.7 us
    pallas_call x1, Pallas kernels, q_proj(): pl.pallas_call(q_kernel, grid=(cols // tile,), in_specs=[pl.BlockSpec((ro...  16.6 us
    pallas_call x1, Pallas kernels, norm_kv(): pl.pallas_call(norm_kv_kernel, grid=(rows // tile,), in_specs=[pl.BlockSp...  15.6 us
  transfers between devices with their start and end apart: 8, of which 3 were waited for; matrix products, arithmetic and copies ran while one was open for 1% of the time, Pallas kernels for 28%

commit v1 on v0

--- a/solution.py
+++ b/solution.py
@@ -11,7 +11,7 @@
 HEAD_DIM = 128
 ROPE_BASE = 4000000
 LN_EPS = 1e-5
-CHUNK = 512
+STRIPS = 4
 LOG2E = 1.4426950408889634
 BF16 = jnp.bfloat16
 F32 = jnp.float32
@@ -37,13 +37,19 @@
 
 
 def norm_kv_kernel(x_ref, gain_ref, wk_ref, wv_ref, cos_ref, sin_ref, h_ref, kv_ref, k_ref, v_ref):
-    x = x_ref[...].astype(F32)
-    width = x.shape[1]
-    mean = jnp.sum(x, axis=1, keepdims=True) * (1.0 / width)
-    centered = x - mean
-    var = jnp.sum(centered * centered, axis=1, keepdims=True) * (1.0 / width)
-    h = (centered * lax.rsqrt(var + LN_EPS) * gain_ref[...].astype(F32)[None, :]).astype(BF16)
-    h_ref[...] = h
+    width = x_ref.shape[1]
+    gain = gain_ref[...].astype(F32)[None, :]
+
+    def normalise(n, carry):
+        rows = pl.ds(pl.multiple_of(n * 16, 16), 16)
+        x = x_ref[rows, :].astype(F32)
+        mean = jnp.sum(x, axis=1, keepdims=True) * (1.0 / width)
+        centered = x - mean
+        var = jnp.sum(centered * centered, axis=1, keepdims=True) * (1.0 / width)
+        h_ref[rows, :] = (centered * lax.rsqrt(var + LN_EPS) * gain).astype(BF16)
+        return carry
+
+    lax.fori_loop(0, x_ref.shape[0] // 16, normalise, 0, unroll=STRIPS)
     k = jnp.dot(h_ref[...], wk_ref[...], preferred_element_type=F32).astype(BF16)
     v = jnp.dot(h_ref[...], wv_ref[...], preferred_element_type=F32).astype(BF16)
     v_ref[...] = v
@@ -91,11 +97,13 @@
 
 
 def q_kernel(h_ref, w_ref, cos_ref, sin_ref, q_ref):
-    q = jnp.dot(h_ref[...], w_ref[...], preferred_element_type=F32).astype(BF16)
-    cosine, sine = cos_ref[...], sin_ref[...]
-    for head in range(q.shape[1] // HEAD_DIM):
-        cols = slice(head * HEAD_DIM, (head + 1) * HEAD_DIM)
-        q_ref[:, cols] = rotate_head(q[:, cols].astype(F32), cosine, sine)
+    for start in range(0, h_ref.shape[0], 512):
+        rows = slice(start, start + 512)
+        q = jnp.dot(h_ref[rows, :], w_ref[...], preferred_element_type=F32).astype(BF16)
+        cosine, sine = cos_ref[rows, :], sin_ref[rows, :]
+        for head in range(q.shape[1] // HEAD_DIM):
+            cols = slice(head * HEAD_DIM, (head + 1) * HEAD_DIM)
+            q_ref[rows, cols] = rotate_head(q[:, cols].astype(F32), cosine, sine)
 
 
 def q_proj(h, wq, cosine, sine):
@@ -118,7 +126,7 @@
     )(h, wq, cosine, sine)
 
 
-def attend_kernel(base, tile, group, blocks, flags_ref, q_ref, *refs):
+def attend_kernel(base, tile, chunk, group, blocks, flags_ref, q_ref, *refs):
     sources = refs[:1 + sum(blocks)]
     o_ref, m_ref, l_ref, acc_ref, s0_ref, s1_ref = refs[1 + sum(blocks):]
     scale2 = (HEAD_DIM ** -0.5) * LOG2E
@@ -127,8 +135,8 @@
     def scores(kv, keys, j, buffer, masked):
         q = q_ref[:, j * HEAD_DIM:(j + 1) * HEAD_DIM]
         top = None
-        for start in range(0, keys, CHUNK):
-            size = min(CHUNK, keys - start)
+        for start in range(0, keys, chunk):
+            size = min(chunk, keys - start)
             s = lax.dot_general(kv[0, start:start + size, :], q, (((1,), (1,)), ((), ())), preferred_element_type=F32)
             if masked and start + size > keys - tile:
                 key = lax.broadcasted_iota(jnp.int32, s.shape, 0) + start
@@ -151,8 +159,8 @@
             if n + 1 < len(items):
                 top8 = scores(items[n + 1][0], keys, items[n + 1][1], buffers[(n + 1) % 2], masked)
             total = part = None
-            for start in range(0, keys, CHUNK):
-                size = min(CHUNK, keys - start)
+            for start in range(0, keys, chunk):
+                size = min(chunk, keys - start)
                 e = jnp.exp2((buffers[n % 2][start:start + size, :] - top) * scale2)
                 e8 = jnp.sum(e.reshape(size // 8, 8, tile), axis=0)
                 vt = jnp.concatenate([kv[1, at:at + HEAD_DIM, :] for at in range(start, start + size, HEAD_DIM)], axis=1)
@@ -188,11 +196,10 @@
         o_ref[:, j * HEAD_DIM:(j + 1) * HEAD_DIM] = out.T.astype(BF16)
 
 
-def attend(flags, q, base, count, groups, sources, blocks):
+def attend(flags, q, base, count, groups, sources, blocks, tile):
     keys = sources[0].shape[2]
     width = q.shape[1] // groups
     group = width // HEAD_DIM
-    tile = 256
     first = base // tile
 
     kv_spec = pl.BlockSpec((None, 2, keys, HEAD_DIM), lambda g, i, f: (g, 0, 0, 0))
@@ -210,7 +217,7 @@
         ],
     )
     return pl.pallas_call(
-        functools.partial(attend_kernel, base, tile, group, blocks),
+        functools.partial(attend_kernel, base, tile, 512, group, blocks),
         grid_spec=grid_spec,
         out_shape=jax.ShapeDtypeStruct((count, q.shape[1]), BF16),
         cost_estimate=cost(10 * count * keys * q.shape[1], 4 * len(sources) * keys * groups * HEAD_DIM, 3 * count * keys * groups * group),
@@ -224,11 +231,11 @@
     a_ref[...] = (gate * jax.nn.sigmoid(gate) * up).astype(BF16)
 
 
-def gate_up(h, wg, wu, first, rows):
-    width, cols = wg.shape
+def gate_up(h, wg, wu, first, rows, col, cols):
+    width = wg.shape[0]
     tile = 512
-    index = first // rows
-    weight_spec = pl.BlockSpec((width, tile), lambda i: (0, i))
+    index, start = first // rows, col // tile
+    weight_spec = pl.BlockSpec((width, tile), lambda i: (0, start + i))
     return pl.pallas_call(
         gate_up_kernel,
         grid=(cols // tile,),
@@ -240,29 +247,44 @@
     )(h, wg, wu)
 
 
-def down_kernel(a_ref, o_ref, wd_ref, wo_ref, out_ref):
-    total = jnp.dot(a_ref[...], wd_ref[...], preferred_element_type=F32)
-    total += jnp.dot(o_ref[...], wo_ref[...], preferred_element_type=F32)
-    out_ref[...] = total.astype(BF16)
-
-
-def down(a, o, wd, wo, a_row, o_row, rows, col, cols):
+def down_kernel(acts, attns, streams, *refs):
+    a_refs, o_refs = refs[:acts], refs[acts:acts + attns]
+    w_refs, wo_ref, out_ref = refs[acts + attns:acts + attns + streams], refs[-2], refs[-1]
+    depth = w_refs[0].shape[0]
+    rows = out_ref.shape[0] // attns
+    a_parts = [a_ref.at[:, start:start + depth] for a_ref in a_refs for start in range(0, a_ref.shape[1], depth)]
+    for n, o_ref in enumerate(o_refs):
+        place = slice(n * rows, (n + 1) * rows)
+        total = jnp.dot(o_ref[...], wo_ref[...], preferred_element_type=F32)
+        for a_part, w_ref in zip(a_parts, w_refs):
+            total += jnp.dot(a_part[place, :], w_ref[...], preferred_element_type=F32)
+        out_ref[place, :] = total.astype(BF16)
+
+
+def down(acts, attns, wd, wo, rows, col, cols):
     tile = 512
     start = col // tile
-    return pl.pallas_call(
-        down_kernel,
+    streams = 4
+    depth = wd.shape[0] // streams
+
+    def act_spec(array, row):
+        return pl.BlockSpec((rows, array.shape[1]), lambda i: (row // rows, 0))
+
+    def stream_spec(n):
+        return pl.BlockSpec((depth, tile), lambda i: (n, start + i))
+
+    return pl.pallas_call(
+        functools.partial(down_kernel, len(acts), len(attns), streams),
         grid=(cols // tile,),
-        in_specs=[
-            pl.BlockSpec((rows, a.shape[1]), lambda i: (a_row // rows, 0)),
-            pl.BlockSpec((rows, o.shape[1]), lambda i: (o_row // rows, 0)),
-            pl.BlockSpec((wd.shape[0], tile), lambda i: (0, start + i)),
-            pl.BlockSpec((wo.shape[0], tile), lambda i: (0, start + i)),
-        ],
+        in_specs=[act_spec(*pair) for pair in acts]
+        + [pl.BlockSpec(o.shape, lambda i: (0, 0)) for o in attns]
+        + [stream_spec(n) for n in range(streams)]
+        + [pl.BlockSpec((wo.shape[0], tile), lambda i: (0, start + i))],
         out_specs=pl.BlockSpec((rows, tile), lambda i: (0, i)),
         out_shape=jax.ShapeDtypeStruct((rows, cols), BF16),
         cost_estimate=cost(2 * rows * (wd.shape[0] + wo.shape[0]) * cols, 2 * cols * (wd.shape[0] + wo.shape[0])),
         name='down',
-    )(a, o, wd, wo)
+    )(*[array for array, _ in acts], *attns, *[wd] * streams, wo)
 
 
 def add_kernel(x_ref, mine_ref, other_ref, *refs):
@@ -272,7 +294,7 @@
 
 def add_chunk(x, mine, other, out, first, col):
     rows, cols = mine.shape
-    tile = min(256, rows)
+    tile = 256
     index, start = first // tile, col // cols
     place = pl.BlockSpec((tile, cols), lambda i: (index + i, start))
     chunk = pl.BlockSpec((tile, cols), lambda i: (i, 0))
@@ -292,15 +314,15 @@
 
 
 SCHEDULE = (
-    ('mlp', 0, 512),
-    ('own', 0, 256),
-    ('down', 0, 256, 0, 3072),
-    ('own', 256, 256),
-    ('down', 256, 256, 0, 3072),
-    ('mlp', 512, 512),
-    ('own', 512, 256),
+    ('mlp', 0, 512, 0, 4096),
+    ('mlp', 512, 512, 0, 1024),
+    ('own', 0, 512, 512),
+    ('down', 0, 512, 0, 1536),
+    ('down', 0, 512, 1536, 1536),
+    ('mlp', 512, 512, 1024, 3072),
+    ('own', 512, 256, 256),
     ('down', 512, 256, 0, 3072),
-    ('own', 768, 256),
+    ('own', 768, 256, 256),
     ('down', 768, 256, 0, 1536),
     ('down', 768, 256, 1536, 1536),
 )
@@ -326,18 +348,19 @@
         for kind, first, rows, *place in SCHEDULE:
             if kind == 'mlp':
                 normed, last = lax.optimization_barrier((normed, last))
-                last = gate_up(normed, w_gate, w_up, first, rows)
-                acts.append((first, last))
+                last = gate_up(normed, w_gate, w_up, first, rows, *place)
+                acts.append((first, rows, last))
             if kind == 'own':
                 q_rot, last = lax.optimization_barrier((q_rot, last))
                 sources = (kv_own, kv_a, kv_b, kv_c)
-                last = attend(flags, q_rot, first, rows, groups, sources, (1, 2))
+                last = attend(flags, q_rot, first, rows, groups, sources, (1, 2), *place)
                 attns.append((first, last))
             if kind == 'down':
                 col, cols = place
-                (a_first, act), (o_first, attn) = [[pair for pair in pairs if pair[0] <= first][-1] for pairs in (acts, attns)]
-                act, last = lax.optimization_barrier((act, last))
-                last = down(act, attn, w_down, w_o, first - a_first, first - o_first, rows, col, cols)
+                act = [(array, first - start) for start, many, array in acts if start <= first < start + many]
+                attn = [array for start, array in attns if first <= start < first + rows]
+                attn, last = lax.optimization_barrier((attn, last))
+                last = down(act, attn, w_down, w_o, rows, col, cols)
                 other = lax.ppermute(last, 'tp', [(0, 1), (1, 0)])
                 pieces.append((last, other, first, col))
         k_own, v_own, last = lax.optimization_barrier((k_own, v_own, last))

time: 372 us -> 372 us (level)
    pallas_call x9 -> x8, Pallas kernels: 148 us -> 143 us  [the longest x5 72.2 us: down(): pl.pallas_call(functools.partial(down_kernel, len(acts), len(attns), stre...]
    pallas_call x2 -> x3, Pallas kernels: 64.8 us -> 69.4 us  [gate_up(): pl.pallas_call(gate_up_kernel, grid=(cols // tile,), in_specs=[pl.BlockSp...]
  transfers between devices with their start and end apart: 8 -> 8, of which waited for: 3 -> 4; matrix products, arithmetic and copies ran while one was open for 1% -> 1% of each run, Pallas kernels for 28% -> 32%
where the time goes in v1:
time: 372 us
  Pallas kernels  262 us (70%)
  waiting for transfers between devices  89.7 us (24%)
  starting transfers between devices  10.3 us (3%)
  other arithmetic  4.38 us (1%)
  local copies, waits for them, and re-layouts  4.28 us (1%)
    pallas_call x5, Pallas kernels, down(): pl.pallas_call(functools.partial(down_kernel, len(acts), len(attns), stre...  72.2 us
    pallas_call x3, Pallas kernels, attend(): pl.pallas_call(functools.partial(attend_kernel, base, tile, 512, group, b...  70.4 us
    pallas_call x3, Pallas kernels, gate_up(): pl.pallas_call(gate_up_kernel, grid=(cols // tile,), in_specs=[pl.BlockSp...  69.4 us
    ppermute x5, waiting for transfers between devices, local_layer(): other = lax.ppermute(last, 'tp', [(0, 1), (1, 0)])  59.8 us
    ppermute x1, waiting for transfers between devices, local_layer(): kv_b = send(kv_own, perm=[(0, 2), (1, 3)])  29.8 us
    pallas_call x1, Pallas kernels, norm_kv(): pl.pallas_call(norm_kv_kernel, grid=(rows // tile,), in_specs=[pl.BlockSp...  17.5 us
    pallas_call x5, Pallas kernels, add_chunk(): pl.pallas_call(add_kernel, grid=(rows // tile,), in_specs=specs, out_spec...  16.6 us
    pallas_call x1, Pallas kernels, q_proj(): pl.pallas_call(q_kernel, grid=(cols // tile,), in_specs=[pl.BlockSpec((ro...  16.2 us
  transfers between devices with their start and end apart: 8, of which 4 were waited for; matrix products, arithmetic and copies ran while one was open for 1% of the time, Pallas kernels for 32%

profile of v1, /device:TPU:3, one launch (start us, length us, event | category | flops | bytes accessed | tf_op | source)
XLA Modules:
  0.0 371.6 jit_solution(6033356516532278740)
XLA Ops:
  0.6 0.7 convert_element_type.10
  1.3 3.0 fusion
  4.4 17.5 %norm_kv.1 = (bf16[1024,3072]{1,0:T(8,128)(2,1)}, bf16[4,2,1024,128]{3,2,1,0:T(8,128)(2,1)}, bf16[1024,512]{1,0:T(8,128)(2,1)}, bf16[1024,512]{1,0:T(8,128)(2,1)}) custom-call(bf16[1024,3072]{1,0:T(8,128)(2,1)} %x_ref.11, bf16[3072]{0:T(1024)(128)(2,1)} %gain_ref.1, bf16[3072,512]{1,0:T(8,128)(2,1)} %wk_ref.1, bf16[3072,512]{1,0:T(8,128)(2,1)} %wv_ref.1, ...), custom_call_target="tpu_custom_call" | custom-call | flops 6442450944 | bytes 18874368 | tf_op jit(solution)/shard_map/norm_kv/pallas_call | solution.py:71
  21.8 1.3 collective-permute-start.1
  23.1 1.3 collective-permute-start
  24.4 16.2 %q_proj.1.q_ref = bf16[1024,1536]{1,0:T(8,128)(2,1)} custom-call(bf16[1024,3072]{1,0:T(8,128)(2,1)} %get-tuple-element.26.h_ref, bf16[3072,1536]{1,0:T(8,128)(2,1)} %w_ref.1, f32[1024,128]{1,0:T(8,128)} %get-tuple-element.36.cos_ref, f32[1024,128]{1,0:T(8,128)} %get-tuple-element.35.sin_ref), custom_call_target="tpu_custom_call" | custom-call | flops 9663676416 | bytes 15728640 | tf_op jit(solution)/shard_map/q_proj/pallas_call | solution.py:113
  40.6 29.8 %collective-permute-done.1.refs_2_ = bf16[4,2,1024,128]{3,2,1,0:T(8,128)(2,1)S(1)} collective-permute-done((bf16[4,2,1024,128]{3,2,1,0:T(8,128)(2,1)}, bf16[4,2,1024,128]{3,2,1,0:T(8,128)(2,1)S(1)}, u32[]{:S(2)}, u32[]{:S(2)}) %collective-permute-start.1) | collective-permute-done | bytes 2097184 | tf_op jit(solution)/shard_map/ppermute | solution.py:341
  70.4 0.0 copy-start.2
  70.4 3.6 collective-permute-start.2
  74.1 32.4 %gate_up.3.refs_0_ = bf16[512,4096]{1,0:T(8,128)(2,1)} custom-call(bf16[1024,3072]{1,0:T(8,128)(2,1)} %get-tuple-element.26.h_ref, bf16[3072,4096]{1,0:T(8,128)(2,1)} %wg_ref.5, bf16[3072,4096]{1,0:T(8,128)(2,1)} %wu_ref.5), custom_call_target="tpu_custom_call" | custom-call | flops 25769803776 | bytes 57671680 | tf_op jit(solution)/shard_map/gate_up/pallas_call | solution.py:239
  106.4 0.0 copy-done.2
  106.4 11.5 %gate_up.4.refs_0_ = bf16[512,1024]{1,0:T(8,128)(2,1)} custom-call(bf16[1024,3072]{1,0:T(8,128)(2,1)} %get-tuple-element.26.h_ref, bf16[3072,4096]{1,0:T(8,128)(2,1)} %wg_ref.5, bf16[3072,4096]{1,0:T(8,128)(2,1)} %wu_ref.5), custom_call_target="tpu_custom_call" | custom-call | flops 6442450944 | bytes 16777216 | tf_op jit(solution)/shard_map/gate_up/pallas_call | solution.py:239
  118.0 0.6 pad_add_fusion.flags_ref
  118.6 0.0 collective-permute-done.refs_1_
  118.6 0.0 collective-permute-done.2.refs_3_
  118.6 30.6 %attend.3.refs_1_ = bf16[512,1536]{1,0:T(8,128)(2,1)} custom-call(s32[2]{0:T(128)} %pad_add_fusion.flags_ref, bf16[1024,1536]{1,0:T(8,128)(2,1)} %q_proj.1.q_ref, bf16[4,2,1024,128]{3,2,1,0:T(8,128)(2,1)} %get-tuple-element.23.refs_0_, bf16[4,2,1024,128]{3,2,1,0:T(8,128)(2,1)} %collective-permute-done.refs_1_, bf16[4,2,1024,128]{3,2,1,0:T(8,128)(2,1)} %copy-done.2, ...), custom_call_target="tpu_custom_call" | custom-call | flops 8053063680 | bytes 8388608 | tf_op jit(solution)/shard_map/attend/pallas_call | solution.py:219
  149.2 15.4 %down.5.mine_ref = bf16[512,1536]{1,0:T(8,128)(2,1)} custom-call(bf16[512,4096]{1,0:T(8,128)(2,1)} %gate_up.3.refs_0_, bf16[512,1536]{1,0:T(8,128)(2,1)} %attend.3.refs_1_, bf16[4096,3072]{1,0:T(8,128)(2,1)} %refs_6_.9, bf16[4096,3072]{1,0:T(8,128)(2,1)} %refs_6_.9, bf16[4096,3072]{1,0:T(8,128)(2,1)} %refs_6_.9, bf16[4096,3072]{1,0:T(8,128)(2,1)} %refs_6_.9, ...), custom_call_target="tpu_custom_call" | custom-call | flops 8858370048 | bytes 17301504 | tf_op jit(solution)/shard_map/down/pallas_call | solution.py:276
  164.6 15.9 %down.6.mine_ref = bf16[512,1536]{1,0:T(8,128)(2,1)} custom-call(bf16[512,4096]{1,0:T(8,128)(2,1)} %gate_up.3.refs_0_, bf16[512,1536]{1,0:T(8,128)(2,1)} %attend.3.refs_1_, bf16[4096,3072]{1,0:T(8,128)(2,1)} %refs_6_.9, bf16[4096,3072]{1,0:T(8,128)(2,1)} %refs_6_.9, bf16[4096,3072]{1,0:T(8,128)(2,1)} %refs_6_.9, bf16[4096,3072]{1,0:T(8,128)(2,1)} %refs_6_.9, ...), custom_call_target="tpu_custom_call" | custom-call | flops 8858370048 | bytes 17301504 | tf_op jit(solution)/shard_map/down/pallas_call | solution.py:276
  180.5 25.5 %gate_up.5.refs_1_ = bf16[512,3072]{1,0:T(8,128)(2,1)} custom-call(bf16[1024,3072]{1,0:T(8,128)(2,1)} %get-tuple-element.26.h_ref, bf16[3072,4096]{1,0:T(8,128)(2,1)} %wg_ref.5, bf16[3072,4096]{1,0:T(8,128)(2,1)} %wu_ref.5), custom_call_target="tpu_custom_call" | custom-call | flops 19327352832 | bytes 44040192 | tf_op jit(solution)/shard_map/gate_up/pallas_call | solution.py:239
  206.0 19.5 %attend.4.refs_2_ = bf16[256,1536]{1,0:T(8,128)(2,1)} custom-call(s32[2]{0:T(128)} %pad_add_fusion.flags_ref, bf16[1024,1536]{1,0:T(8,128)(2,1)} %q_proj.1.q_ref, bf16[4,2,1024,128]{3,2,1,0:T(8,128)(2,1)} %get-tuple-element.23.refs_0_, bf16[4,2,1024,128]{3,2,1,0:T(8,128)(2,1)} %collective-permute-done.refs_1_, bf16[4,2,1024,128]{3,2,1,0:T(8,128)(2,1)} %copy-done.2, ...), custom_call_target="tpu_custom_call" | custom-call | flops 4026531840 | bytes 8388608 | tf_op jit(solution)/shard_map/attend/pallas_call | solution.py:219
  225.5 0.0 copy-start
  225.5 0.0 copy-start.1
  225.5 17.8 %down.7.mine_ref = bf16[256,3072]{1,0:T(8,128)(2,1)} custom-call(bf16[512,1024]{1,0:T(8,128)(2,1)} %gate_up.4.refs_0_, bf16[512,3072]{1,0:T(8,128)(2,1)} %gate_up.5.refs_1_, bf16[256,1536]{1,0:T(8,128)(2,1)} %attend.4.refs_2_, bf16[4096,3072]{1,0:T(8,128)(2,1)} %refs_6_.9, bf16[4096,3072]{1,0:T(8,128)(2,1)} %refs_6_.9, bf16[4096,3072]{1,0:T(8,128)(2,1)} %refs_6_.9, ...), custom_call_target="tpu_custom_call" | custom-call | flops 8858370048 | bytes 34603008 | tf_op jit(solution)/shard_map/down/pallas_call | solution.py:276
  243.4 1.2 collective-permute-start.5
  244.6 0.0 copy-done
  244.6 0.2 collective-permute-start.6
  244.8 0.0 copy-done.1
  244.8 1.2 collective-permute-start.7
  246.1 20.3 %attend.5.refs_2_ = bf16[256,1536]{1,0:T(8,128)(2,1)} custom-call(s32[2]{0:T(128)} %pad_add_fusion.flags_ref, bf16[1024,1536]{1,0:T(8,128)(2,1)} %q_proj.1.q_ref, bf16[4,2,1024,128]{3,2,1,0:T(8,128)(2,1)} %get-tuple-element.23.refs_0_, bf16[4,2,1024,128]{3,2,1,0:T(8,128)(2,1)} %collective-permute-done.refs_1_, bf16[4,2,1024,128]{3,2,1,0:T(8,128)(2,1)} %copy-done.2, ...), custom_call_target="tpu_custom_call" | custom-call | flops 4026531840 | bytes 8388608 | tf_op jit(solution)/shard_map/attend/pallas_call | solution.py:219
  266.3 11.4 %down.8.mine_ref = bf16[256,1536]{1,0:T(8,128)(2,1)} custom-call(bf16[512,1024]{1,0:T(8,128)(2,1)} %gate_up.4.refs_0_, bf16[512,3072]{1,0:T(8,128)(2,1)} %gate_up.5.refs_1_, bf16[256,1536]{1,0:T(8,128)(2,1)} %attend.5.refs_2_, bf16[4096,3072]{1,0:T(8,128)(2,1)} %refs_6_.9, bf16[4096,3072]{1,0:T(8,128)(2,1)} %refs_6_.9, bf16[4096,3072]{1,0:T(8,128)(2,1)} %refs_6_.9, ...), custom_call_target="tpu_custom_call" | custom-call | flops 4429185024 | bytes 17301504 | tf_op jit(solution)/shard_map/down/pallas_call | solution.py:276
  277.7 0.2 collective-permute-start.4
  277.9 11.7 %down.9.mine_ref = bf16[256,1536]{1,0:T(8,128)(2,1)} custom-call(bf16[512,1024]{1,0:T(8,128)(2,1)} %gate_up.4.refs_0_, bf16[512,3072]{1,0:T(8,128)(2,1)} %gate_up.5.refs_1_, bf16[256,1536]{1,0:T(8,128)(2,1)} %attend.5.refs_2_, bf16[4096,3072]{1,0:T(8,128)(2,1)} %refs_6_.9, bf16[4096,3072]{1,0:T(8,128)(2,1)} %refs_6_.9, bf16[4096,3072]{1,0:T(8,128)(2,1)} %refs_6_.9, ...), custom_call_target="tpu_custom_call" | custom-call | flops 4429185024 | bytes 17301504 | tf_op jit(solution)/shard_map/down/pallas_call | solution.py:276
  289.7 1.2 collective-permute-start.3
  290.9 2.1 reshape.42
  293.0 2.1 reshape.43
  295.2 52.3 %collective-permute-done.7.other_ref = bf16[512,1536]{1,0:T(8,128)(2,1)} collective-permute-done((bf16[512,1536]{1,0:T(8,128)(2,1)S(1)}, bf16[512,1536]{1,0:T(8,128)(2,1)}, u32[]{:S(2)}, u32[]{:S(2)}) %collective-permute-start.7) | collective-permute-done | bytes 1572896 | tf_op jit(solution)/shard_map/ppermute | solution.py:364
  347.5 3.5 add.32.refs_0_
  351.0 0.0 collective-permute-done.6.other_ref
  351.0 3.5 add.33.refs_0_
  354.5 0.0 collective-permute-done.5.other_ref
  354.5 4.1 %add.34.refs_0_ = bf16[1024,3072]{1,0:T(8,128)(2,1)} custom-call(bf16[1024,3072]{1,0:T(8,128)(2,1)} %x_ref.11, bf16[256,3072]{1,0:T(8,128)(2,1)} %down.7.mine_ref, bf16[256,3072]{1,0:T(8,128)(2,1)} %collective-permute-done.5.other_ref, bf16[1024,3072]{1,0:T(8,128)(2,1)} %add.33.refs_0_), custom_call_target="tpu_custom_call", output_to_operand_aliasing={{}: (3, {})} | custom-call | flops 2359296 | bytes 6291456 | tf_op jit(solution)/shard_map/add/pallas_call | solution.py:304
  358.5 1.8 collective-permute-done.4.other_ref
  360.4 2.8 add.35.refs_0_
  363.1 5.7 %collective-permute-done.3.other_ref = bf16[256,1536]{1,0:T(8,128)(2,1)} collective-permute-done((bf16[256,1536]{1,0:T(8,128)(2,1)}, bf16[256,1536]{1,0:T(8,128)(2,1)}, u32[]{:S(2)}, u32[]{:S(2)}) %collective-permute-start.3) | collective-permute-done | bytes 786464 | tf_op jit(solution)/shard_map/ppermute | solution.py:364
  368.8 2.8 add.36
  (1 shorter events, 0.0 us)
Async XLA Ops:
  21.8 48.6 %collective-permute-start.1 = (bf16[4,2,1024,128]{3,2,1,0:T(8,128)(2,1)}, bf16[4,2,1024,128]{3,2,1,0:T(8,128)(2,1)S(1)}, u32[]{:S(2)}, u32[]{:S(2)}) collective-permute-start(bf16[4,2,1024,128]{3,2,1,0:T(8,128)(2,1)} %get-tuple-element.23.refs_0_), channel_id=1, source_target_pairs={{0,2},{1,3},{4,6},{5,7}} | collective-permute-start | bytes 6291464 | tf_op jit(solution)/shard_map/ppermute | solution.py:341
  23.1 95.5 %collective-permute-start = (bf16[4,2,1024,128]{3,2,1,0:T(8,128)(2,1)}, bf16[4,2,1024,128]{3,2,1,0:T(8,128)(2,1)}, u32[]{:S(2)}, u32[]{:S(2)}) collective-permute-start(bf16[4,2,1024,128]{3,2,1,0:T(8,128)(2,1)} %get-tuple-element.23.refs_0_), channel_id=1, source_target_pairs={{0,1},{2,3},{4,5},{6,7}} | collective-permute-start | bytes 6291464 | tf_op jit(solution)/shard_map/ppermute | solution.py:342
  70.4 36.0 %copy-start.2 = (bf16[4,2,1024,128]{3,2,1,0:T(8,128)(2,1)}, bf16[4,2,1024,128]{3,2,1,0:T(8,128)(2,1)S(1)}, u32[]{:S(2)}) copy-start(bf16[4,2,1024,128]{3,2,1,0:T(8,128)(2,1)S(1)} %collective-permute-done.1.refs_2_) | copy-start | bytes 6291460
  70.4 48.2 %collective-permute-start.2 = (bf16[4,2,1024,128]{3,2,1,0:T(8,128)(2,1)S(1)}, bf16[4,2,1024,128]{3,2,1,0:T(8,128)(2,1)}, u32[]{:S(2)}, u32[]{:S(2)}) collective-permute-start(bf16[4,2,1024,128]{3,2,1,0:T(8,128)(2,1)S(1)} %collective-permute-done.1.refs_2_), channel_id=1, source_target_pairs={{2,3},{3,2},{6,7},{7,6}} | collective-permute-start | bytes 6291464 | tf_op jit(solution)/shard_map/ppermute | solution.py:343
  225.5 19.1 %copy-start = (bf16[512,1536]{1,0:T(8,128)(2,1)S(1)}, bf16[512,1536]{1,0:T(8,128)(2,1)}, u32[]{:S(2)}) copy-start(bf16[512,1536]{1,0:T(8,128)(2,1)} %down.6.mine_ref) | copy-start | bytes 4718596
  225.5 19.3 %copy-start.1 = (bf16[512,1536]{1,0:T(8,128)(2,1)S(1)}, bf16[512,1536]{1,0:T(8,128)(2,1)}, u32[]{:S(2)}) copy-start(bf16[512,1536]{1,0:T(8,128)(2,1)} %down.5.mine_ref) | copy-start | bytes 4718596
  243.4 111.1 %collective-permute-start.5 = (bf16[256,3072]{1,0:T(8,128)(2,1)}, bf16[256,3072]{1,0:T(8,128)(2,1)}, u32[]{:S(2)}, u32[]{:S(2)}) collective-permute-start(bf16[256,3072]{1,0:T(8,128)(2,1)} %down.7.mine_ref), channel_id=1, source_target_pairs={{0,4},{4,0},{1,5},{5,1},{2,6},{6,2},{3,7},{7,3}} | collective-permute-start | bytes 4718600 | tf_op jit(solution)/shard_map/ppermute | solution.py:364
  244.6 106.4 %collective-permute-start.6 = (bf16[512,1536]{1,0:T(8,128)(2,1)S(1)}, bf16[512,1536]{1,0:T(8,128)(2,1)}, u32[]{:S(2)}, u32[]{:S(2)}) collective-permute-start(bf16[512,1536]{1,0:T(8,128)(2,1)S(1)} %copy-done), channel_id=1, source_target_pairs={{0,4},{4,0},{1,5},{5,1},{2,6},{6,2},{3,7},{7,3}} | collective-permute-start | bytes 4718600 | tf_op jit(solution)/shard_map/ppermute | solution.py:364
  244.8 102.7 %collective-permute-start.7 = (bf16[512,1536]{1,0:T(8,128)(2,1)S(1)}, bf16[512,1536]{1,0:T(8,128)(2,1)}, u32[]{:S(2)}, u32[]{:S(2)}) collective-permute-start(bf16[512,1536]{1,0:T(8,128)(2,1)S(1)} %copy-done.1), channel_id=1, source_target_pairs={{0,4},{4,0},{1,5},{5,1},{2,6},{6,2},{3,7},{7,3}} | collective-permute-start | bytes 4718600 | tf_op jit(solution)/shard_map/ppermute | solution.py:364
  277.7 82.7 %collective-permute-start.4 = (bf16[256,1536]{1,0:T(8,128)(2,1)}, bf16[256,1536]{1,0:T(8,128)(2,1)}, u32[]{:S(2)}, u32[]{:S(2)}) collective-permute-start(bf16[256,1536]{1,0:T(8,128)(2,1)} %down.8.mine_ref), channel_id=1, source_target_pairs={{0,4},{4,0},{1,5},{5,1},{2,6},{6,2},{3,7},{7,3}} | collective-permute-start | bytes 2359304 | tf_op jit(solution)/shard_map/ppermute | solution.py:364
  289.7 79.1 %collective-permute-start.3 = (bf16[256,1536]{1,0:T(8,128)(2,1)}, bf16[256,1536]{1,0:T(8,128)(2,1)}, u32[]{:S(2)}, u32[]{:S(2)}) collective-permute-start(bf16[256,1536]{1,0:T(8,128)(2,1)} %down.9.mine_ref), channel_id=1, source_target_pairs={{0,4},{4,0},{1,5},{5,1},{2,6},{6,2},{3,7},{7,3}} | collective-permute-start | bytes 2359304 | tf_op jit(solution)/shard_map/ppermute | solution.py:364

commit v2 on v1

--- a/solution.py
+++ b/solution.py
@@ -11,7 +11,6 @@
 HEAD_DIM = 128
 ROPE_BASE = 4000000
 LN_EPS = 1e-5
-STRIPS = 4
 LOG2E = 1.4426950408889634
 BF16 = jnp.bfloat16
 F32 = jnp.float32
@@ -37,19 +36,12 @@
 
 
 def norm_kv_kernel(x_ref, gain_ref, wk_ref, wv_ref, cos_ref, sin_ref, h_ref, kv_ref, k_ref, v_ref):
-    width = x_ref.shape[1]
-    gain = gain_ref[...].astype(F32)[None, :]
-
-    def normalise(n, carry):
-        rows = pl.ds(pl.multiple_of(n * 16, 16), 16)
-        x = x_ref[rows, :].astype(F32)
-        mean = jnp.sum(x, axis=1, keepdims=True) * (1.0 / width)
-        centered = x - mean
-        var = jnp.sum(centered * centered, axis=1, keepdims=True) * (1.0 / width)
-        h_ref[rows, :] = (centered * lax.rsqrt(var + LN_EPS) * gain).astype(BF16)
-        return carry
-
-    lax.fori_loop(0, x_ref.shape[0] // 16, normalise, 0, unroll=STRIPS)
+    x = x_ref[...].astype(F32)
+    width = x.shape[1]
+    mean = jnp.sum(x, axis=1, keepdims=True) * (1.0 / width)
+    centered = x - mean
+    var = jnp.sum(centered * centered, axis=1, keepdims=True) * (1.0 / width)
+    h_ref[...] = (centered * lax.rsqrt(var + LN_EPS) * gain_ref[...].astype(F32)[None, :]).astype(BF16)
     k = jnp.dot(h_ref[...], wk_ref[...], preferred_element_type=F32).astype(BF16)
     v = jnp.dot(h_ref[...], wv_ref[...], preferred_element_type=F32).astype(BF16)
     v_ref[...] = v
@@ -264,7 +256,7 @@
 def down(acts, attns, wd, wo, rows, col, cols):
     tile = 512
     start = col // tile
-    streams = 4
+    streams = 1
     depth = wd.shape[0] // streams
 
     def act_spec(array, row):
@@ -315,16 +307,12 @@
 
 SCHEDULE = (
     ('mlp', 0, 512, 0, 4096),
-    ('mlp', 512, 512, 0, 1024),
     ('own', 0, 512, 512),
-    ('down', 0, 512, 0, 1536),
-    ('down', 0, 512, 1536, 1536),
-    ('mlp', 512, 512, 1024, 3072),
-    ('own', 512, 256, 256),
-    ('down', 512, 256, 0, 3072),
-    ('own', 768, 256, 256),
-    ('down', 768, 256, 0, 1536),
-    ('down', 768, 256, 1536, 1536),
+    ('down', 0, 512, 0, 3072),
+    ('mlp', 512, 512, 0, 4096),
+    ('own', 512, 512, 512),
+    ('down', 512, 512, 0, 1536),
+    ('down', 512, 512, 1536, 1536),
 )
 
 
@@ -341,6 +329,8 @@
         kv_b = send(kv_own, perm=[(0, 2), (1, 3)])
         kv_a = send(kv_own, perm=[(0, 1), (2, 3)])
         kv_c = send(kv_b, perm=[(2, 3), (3, 2)])
+        cache_shape = (k_own.shape[0], groups, HEAD_DIM)
+        k_cache, v_cache = k_own.reshape(cache_shape), v_own.reshape(cache_shape)
         flags = jnp.stack([me % 2, me // 2]).astype(jnp.int32)
         q_rot = q_proj(normed, w_q, cosine, sine)
         last = q_rot
@@ -363,9 +353,6 @@
                 last = down(act, attn, w_down, w_o, rows, col, cols)
                 other = lax.ppermute(last, 'tp', [(0, 1), (1, 0)])
                 pieces.append((last, other, first, col))
-        k_own, v_own, last = lax.optimization_barrier((k_own, v_own, last))
-        cache_shape = (k_own.shape[0], groups, HEAD_DIM)
-        k_cache, v_cache = k_own.reshape(cache_shape), v_own.reshape(cache_shape)
         hidden_out = None
         for part, other, first, col in pieces:
             hidden_out = add_chunk(hidden, part, other, hidden_out, first, col)

time: 372 us -> 301 us (0.81)
  waiting for transfers between devices: 89.7 us -> 53.8 us
  Pallas kernels: 262 us -> 227 us
    ppermute x5 -> x3, waiting for transfers between devices: 59.8 us -> 24 us  [local_layer(): other = lax.ppermute(last, 'tp', [(0, 1), (1, 0)])]
    pallas_call x5 -> x3, Pallas kernels: 72.2 us -> 53.6 us  [down(): pl.pallas_call(functools.partial(down_kernel, len(acts), len(attns), stre...]
    pallas_call x3 -> x2, Pallas kernels: 70.4 us -> 64.7 us  [attend(): pl.pallas_call(functools.partial(attend_kernel, base, tile, 512, group, b...]
    pallas_call x3 -> x2, Pallas kernels: 69.4 us -> 64.7 us  [gate_up(): pl.pallas_call(gate_up_kernel, grid=(cols // tile,), in_specs=[pl.BlockSp...]
    pallas_call x5 -> x3, Pallas kernels: 16.6 us -> 12.4 us  [add_chunk(): pl.pallas_call(add_kernel, grid=(rows // tile,), in_specs=specs, out_spec...]
  transfers between devices with their start and end apart: 8 -> 6, of which waited for: 4 -> 3; matrix products, arithmetic and copies ran while one was open for 1% -> 2% of each run, Pallas kernels for 32% -> 51%
where the time goes in v2:
time: 301 us
  Pallas kernels  227 us (75%)
  waiting for transfers between devices  53.8 us (18%)
  starting transfers between devices  8.88 us (3%)
  local copies, waits for them, and re-layouts  5.9 us (2%)
  other arithmetic  4.3 us (1%)
    pallas_call x2, Pallas kernels, attend(): pl.pallas_call(functools.partial(attend_kernel, base, tile, 512, group, b...  64.7 us
    pallas_call x2, Pallas kernels, gate_up(): pl.pallas_call(gate_up_kernel, grid=(cols // tile,), in_specs=[pl.BlockSp...  64.7 us
    pallas_call x3, Pallas kernels, down(): pl.pallas_call(functools.partial(down_kernel, len(acts), len(attns), stre...  53.6 us
    ppermute x1, waiting for transfers between devices, local_layer(): kv_b = send(kv_own, perm=[(0, 2), (1, 3)])  29.8 us
    ppermute x3, waiting for transfers between devices, local_layer(): other = lax.ppermute(last, 'tp', [(0, 1), (1, 0)])  24 us
    pallas_call x1, Pallas kernels, q_proj(): pl.pallas_call(q_kernel, grid=(cols // tile,), in_specs=[pl.BlockSpec((ro...  16.2 us
    pallas_call x1, Pallas kernels, norm_kv(): pl.pallas_call(norm_kv_kernel, grid=(rows // tile,), in_specs=[pl.BlockSp...  15.6 us
    pallas_call x3, Pallas kernels, add_chunk(): pl.pallas_call(add_kernel, grid=(rows // tile,), in_specs=specs, out_spec...  12.4 us
  transfers between devices with their start and end apart: 6, of which 3 were waited for; matrix products, arithmetic and copies ran while one was open for 2% of the time, Pallas kernels for 51%

profile of v2, /device:TPU:3, one launch (start us, length us, event | category | flops | bytes accessed | tf_op | source)
XLA Modules:
  0.0 300.8 jit_solution(18278089785628541130)
XLA Ops:
  0.6 0.7 convert_element_type.10
  1.3 3.0 %fusion = (f32[1024,128]{1,0:T(8,128)}, f32[1024,128]{1,0:T(8,128)}) fusion(f32[128]{0:T(128)S(1)} %get-tuple-element.25, f32[128]{0:T(128)S(1)} %get-tuple-element.26, f32[1024]{0:T(1024)S(1)} %convert_element_type.10), kind=kLoop, calls=%fused_computation.2 | loop fusion | flops 262144 | bytes 1053696 | tf_op jit(solution)/shard_map/mul | solution.py:29
  4.4 15.6 %norm_kv.1 = (bf16[1024,3072]{1,0:T(8,128)(2,1)}, bf16[4,2,1024,128]{3,2,1,0:T(8,128)(2,1)}, bf16[1024,512]{1,0:T(8,128)(2,1)}, bf16[1024,512]{1,0:T(8,128)(2,1)}) custom-call(bf16[1024,3072]{1,0:T(8,128)(2,1)} %x_ref.7, bf16[3072]{0:T(1024)(128)(2,1)} %gain_ref.1, bf16[3072,512]{1,0:T(8,128)(2,1)} %wk_ref.1, bf16[3072,512]{1,0:T(8,128)(2,1)} %wv_ref.1, ...), custom_call_target="tpu_custom_call" | custom-call | flops 6442450944 | bytes 18874368 | tf_op jit(solution)/shard_map/norm_kv/pallas_call | solution.py:63
  19.9 1.3 collective-permute-start.1
  21.2 1.3 collective-permute-start
  22.5 16.2 %q_proj.1.q_ref = bf16[1024,1536]{1,0:T(8,128)(2,1)} custom-call(bf16[1024,3072]{1,0:T(8,128)(2,1)} %get-tuple-element.17.h_ref, bf16[3072,1536]{1,0:T(8,128)(2,1)} %w_ref.1, f32[1024,128]{1,0:T(8,128)} %get-tuple-element.24.cos_ref, f32[1024,128]{1,0:T(8,128)} %get-tuple-element.23.sin_ref), custom_call_target="tpu_custom_call" | custom-call | flops 9663676416 | bytes 15728640 | tf_op jit(solution)/shard_map/q_proj/pallas_call | solution.py:105
  38.8 29.8 %collective-permute-done.1.refs_2_ = bf16[4,2,1024,128]{3,2,1,0:T(8,128)(2,1)S(1)} collective-permute-done((bf16[4,2,1024,128]{3,2,1,0:T(8,128)(2,1)}, bf16[4,2,1024,128]{3,2,1,0:T(8,128)(2,1)S(1)}, u32[]{:S(2)}, u32[]{:S(2)}) %collective-permute-start.1) | collective-permute-done | bytes 2097184 | tf_op jit(solution)/shard_map/ppermute | solution.py:329
  68.5 0.0 copy-start.1
  68.5 3.6 %collective-permute-start.2 = (bf16[4,2,1024,128]{3,2,1,0:T(8,128)(2,1)S(1)}, bf16[4,2,1024,128]{3,2,1,0:T(8,128)(2,1)}, u32[]{:S(2)}, u32[]{:S(2)}) collective-permute-start(bf16[4,2,1024,128]{3,2,1,0:T(8,128)(2,1)S(1)} %collective-permute-done.1.refs_2_), channel_id=1, source_target_pairs={{2,3},{3,2},{6,7},{7,6}} | collective-permute-start | bytes 6291464 | tf_op jit(solution)/shard_map/ppermute | solution.py:331
  72.2 32.4 %gate_up.2.refs_0_ = bf16[512,4096]{1,0:T(8,128)(2,1)} custom-call(bf16[1024,3072]{1,0:T(8,128)(2,1)} %get-tuple-element.17.h_ref, bf16[3072,4096]{1,0:T(8,128)(2,1)} %wg_ref.3, bf16[3072,4096]{1,0:T(8,128)(2,1)} %wu_ref.3), custom_call_target="tpu_custom_call" | custom-call | flops 25769803776 | bytes 57671680 | tf_op jit(solution)/shard_map/gate_up/pallas_call | solution.py:231
  104.5 0.0 copy-done.1
  104.5 0.6 pad_add_fusion.flags_ref
  105.1 0.0 collective-permute-done.refs_1_
  105.1 0.0 collective-permute-done.2.refs_3_
  105.1 30.6 %attend.2.refs_1_ = bf16[512,1536]{1,0:T(8,128)(2,1)} custom-call(s32[2]{0:T(128)} %pad_add_fusion.flags_ref, bf16[1024,1536]{1,0:T(8,128)(2,1)} %q_proj.1.q_ref, bf16[4,2,1024,128]{3,2,1,0:T(8,128)(2,1)} %get-tuple-element.16.refs_0_, bf16[4,2,1024,128]{3,2,1,0:T(8,128)(2,1)} %collective-permute-done.refs_1_, bf16[4,2,1024,128]{3,2,1,0:T(8,128)(2,1)} %copy-done.1, ...), custom_call_target="tpu_custom_call" | custom-call | flops 8053063680 | bytes 8388608 | tf_op jit(solution)/shard_map/attend/pallas_call | solution.py:211
  135.7 24.2 %down.3.mine_ref = bf16[512,3072]{1,0:T(8,128)(2,1)} custom-call(bf16[512,4096]{1,0:T(8,128)(2,1)} %gate_up.2.refs_0_, bf16[512,1536]{1,0:T(8,128)(2,1)} %attend.2.refs_1_, bf16[4096,3072]{1,0:T(8,128)(2,1)} %refs_2_.5, bf16[1536,3072]{1,0:T(8,128)(2,1)} %refs_3_.5), custom_call_target="tpu_custom_call" | custom-call | flops 17716740096 | bytes 34603008 | tf_op jit(solution)/shard_map/down/pallas_call | solution.py:268
  159.9 1.2 collective-permute-start.5
  161.2 32.3 %gate_up.3.refs_0_ = bf16[512,4096]{1,0:T(8,128)(2,1)} custom-call(bf16[1024,3072]{1,0:T(8,128)(2,1)} %get-tuple-element.17.h_ref, bf16[3072,4096]{1,0:T(8,128)(2,1)} %wg_ref.3, bf16[3072,4096]{1,0:T(8,128)(2,1)} %wu_ref.3), custom_call_target="tpu_custom_call" | custom-call | flops 25769803776 | bytes 57671680 | tf_op jit(solution)/shard_map/gate_up/pallas_call | solution.py:231
  193.5 34.1 %attend.3.refs_1_ = bf16[512,1536]{1,0:T(8,128)(2,1)} custom-call(s32[2]{0:T(128)} %pad_add_fusion.flags_ref, bf16[1024,1536]{1,0:T(8,128)(2,1)} %q_proj.1.q_ref, bf16[4,2,1024,128]{3,2,1,0:T(8,128)(2,1)} %get-tuple-element.16.refs_0_, bf16[4,2,1024,128]{3,2,1,0:T(8,128)(2,1)} %collective-permute-done.refs_1_, bf16[4,2,1024,128]{3,2,1,0:T(8,128)(2,1)} %copy-done.1, ...), custom_call_target="tpu_custom_call" | custom-call | flops 8053063680 | bytes 8388608 | tf_op jit(solution)/shard_map/attend/pallas_call | solution.py:211
  227.6 14.7 %down.4.mine_ref = bf16[512,1536]{1,0:T(8,128)(2,1)} custom-call(bf16[512,4096]{1,0:T(8,128)(2,1)} %gate_up.3.refs_0_, bf16[512,1536]{1,0:T(8,128)(2,1)} %attend.3.refs_1_, bf16[4096,3072]{1,0:T(8,128)(2,1)} %refs_2_.5, bf16[1536,3072]{1,0:T(8,128)(2,1)} %refs_3_.5), custom_call_target="tpu_custom_call" | custom-call | flops 8858370048 | bytes 17301504 | tf_op jit(solution)/shard_map/down/pallas_call | solution.py:268
  242.3 0.2 collective-permute-start.4
  242.5 14.7 %down.5.mine_ref = bf16[512,1536]{1,0:T(8,128)(2,1)} custom-call(bf16[512,4096]{1,0:T(8,128)(2,1)} %gate_up.3.refs_0_, bf16[512,1536]{1,0:T(8,128)(2,1)} %attend.3.refs_1_, bf16[4096,3072]{1,0:T(8,128)(2,1)} %refs_2_.5, bf16[1536,3072]{1,0:T(8,128)(2,1)} %refs_3_.5), custom_call_target="tpu_custom_call" | custom-call | flops 8858370048 | bytes 17301504 | tf_op jit(solution)/shard_map/down/pallas_call | solution.py:268
  257.2 1.2 collective-permute-start.3
  258.4 2.1 reshape.42
  260.6 2.1 reshape.43
  262.7 0.0 collective-permute-done.5.other_ref
  262.7 0.0 copy-start
  262.7 1.6 copy-done
  264.3 5.4 %add.30.refs_0_ = bf16[1024,3072]{1,0:T(8,128)(2,1)} custom-call(bf16[1024,3072]{1,0:T(8,128)(2,1)} %x_ref.7, bf16[512,3072]{1,0:T(8,128)(2,1)} %down.3.mine_ref, bf16[512,3072]{1,0:T(8,128)(2,1)} %copy-done), custom_call_target="tpu_custom_call" | custom-call | flops 4718592 | bytes 12582912 | tf_op jit(solution)/shard_map/add/pallas_call | solution.py:296
  269.8 9.2 %collective-permute-done.4.other_ref = bf16[512,1536]{1,0:T(8,128)(2,1)} collective-permute-done((bf16[512,1536]{1,0:T(8,128)(2,1)}, bf16[512,1536]{1,0:T(8,128)(2,1)}, u32[]{:S(2)}, u32[]{:S(2)}) %collective-permute-start.4) | collective-permute-done | bytes 1572896 | tf_op jit(solution)/shard_map/ppermute | solution.py:354
  279.0 3.5 %add.31.refs_0_ = bf16[1024,3072]{1,0:T(8,128)(2,1)} custom-call(bf16[1024,3072]{1,0:T(8,128)(2,1)} %x_ref.7, bf16[512,1536]{1,0:T(8,128)(2,1)} %down.4.mine_ref, bf16[512,1536]{1,0:T(8,128)(2,1)} %collective-permute-done.4.other_ref, bf16[1024,3072]{1,0:T(8,128)(2,1)} %add.30.refs_0_), custom_call_target="tpu_custom_call", output_to_operand_aliasing={{}: (3, {})} | custom-call | flops 2359296 | bytes 6291456 | tf_op jit(solution)/shard_map/add/pallas_call | solution.py:296
  282.5 14.8 %collective-permute-done.3.other_ref = bf16[512,1536]{1,0:T(8,128)(2,1)} collective-permute-done((bf16[512,1536]{1,0:T(8,128)(2,1)}, bf16[512,1536]{1,0:T(8,128)(2,1)}, u32[]{:S(2)}, u32[]{:S(2)}) %collective-permute-start.3) | collective-permute-done | bytes 1572896 | tf_op jit(solution)/shard_map/ppermute | solution.py:354
  297.3 3.5 %add.32 = bf16[1024,3072]{1,0:T(8,128)(2,1)} custom-call(bf16[1024,3072]{1,0:T(8,128)(2,1)} %x_ref.7, bf16[512,1536]{1,0:T(8,128)(2,1)} %down.5.mine_ref, bf16[512,1536]{1,0:T(8,128)(2,1)} %collective-permute-done.3.other_ref, bf16[1024,3072]{1,0:T(8,128)(2,1)} %add.31.refs_0_), custom_call_target="tpu_custom_call", output_to_operand_aliasing={{}: (3, {})} | custom-call | flops 2359296 | bytes 6291456 | tf_op jit(solution)/shard_map/add/pallas_call | solution.py:296
  (1 shorter events, 0.0 us)
Async XLA Ops:
  19.9 48.6 %collective-permute-start.1 = (bf16[4,2,1024,128]{3,2,1,0:T(8,128)(2,1)}, bf16[4,2,1024,128]{3,2,1,0:T(8,128)(2,1)S(1)}, u32[]{:S(2)}, u32[]{:S(2)}) collective-permute-start(bf16[4,2,1024,128]{3,2,1,0:T(8,128)(2,1)} %get-tuple-element.16.refs_0_), channel_id=1, source_target_pairs={{0,2},{1,3},{4,6},{5,7}} | collective-permute-start | bytes 6291464 | tf_op jit(solution)/shard_map/ppermute | solution.py:329
  21.2 83.9 %collective-permute-start = (bf16[4,2,1024,128]{3,2,1,0:T(8,128)(2,1)}, bf16[4,2,1024,128]{3,2,1,0:T(8,128)(2,1)}, u32[]{:S(2)}, u32[]{:S(2)}) collective-permute-start(bf16[4,2,1024,128]{3,2,1,0:T(8,128)(2,1)} %get-tuple-element.16.refs_0_), channel_id=1, source_target_pairs={{0,1},{2,3},{4,5},{6,7}} | collective-permute-start | bytes 6291464 | tf_op jit(solution)/shard_map/ppermute | solution.py:330
  68.5 36.0 %copy-start.1 = (bf16[4,2,1024,128]{3,2,1,0:T(8,128)(2,1)}, bf16[4,2,1024,128]{3,2,1,0:T(8,128)(2,1)S(1)}, u32[]{:S(2)}) copy-start(bf16[4,2,1024,128]{3,2,1,0:T(8,128)(2,1)S(1)} %collective-permute-done.1.refs_2_) | copy-start | bytes 6291460
  68.5 36.5 %collective-permute-start.2 = (bf16[4,2,1024,128]{3,2,1,0:T(8,128)(2,1)S(1)}, bf16[4,2,1024,128]{3,2,1,0:T(8,128)(2,1)}, u32[]{:S(2)}, u32[]{:S(2)}) collective-permute-start(bf16[4,2,1024,128]{3,2,1,0:T(8,128)(2,1)S(1)} %collective-permute-done.1.refs_2_), channel_id=1, source_target_pairs={{2,3},{3,2},{6,7},{7,6}} | collective-permute-start | bytes 6291464 | tf_op jit(solution)/shard_map/ppermute | solution.py:331
  159.9 102.8 %collective-permute-start.5 = (bf16[512,3072]{1,0:T(8,128)(2,1)}, bf16[512,3072]{1,0:T(8,128)(2,1)S(1)}, u32[]{:S(2)}, u32[]{:S(2)}) collective-permute-start(bf16[512,3072]{1,0:T(8,128)(2,1)} %down.3.mine_ref), channel_id=1, source_target_pairs={{0,4},{4,0},{1,5},{5,1},{2,6},{6,2},{3,7},{7,3}} | collective-permute-start | bytes 9437192 | tf_op jit(solution)/shard_map/ppermute | solution.py:354
  242.3 36.7 %collective-permute-start.4 = (bf16[512,1536]{1,0:T(8,128)(2,1)}, bf16[512,1536]{1,0:T(8,128)(2,1)}, u32[]{:S(2)}, u32[]{:S(2)}) collective-permute-start(bf16[512,1536]{1,0:T(8,128)(2,1)} %down.4.mine_ref), channel_id=1, source_target_pairs={{0,4},{4,0},{1,5},{5,1},{2,6},{6,2},{3,7},{7,3}} | collective-permute-start | bytes 4718600 | tf_op jit(solution)/shard_map/ppermute | solution.py:354
  257.2 40.1 %collective-permute-start.3 = (bf16[512,1536]{1,0:T(8,128)(2,1)}, bf16[512,1536]{1,0:T(8,128)(2,1)}, u32[]{:S(2)}, u32[]{:S(2)}) collective-permute-start(bf16[512,1536]{1,0:T(8,128)(2,1)} %down.5.mine_ref), channel_id=1, source_target_pairs={{0,4},{4,0},{1,5},{5,1},{2,6},{6,2},{3,7},{7,3}} | collective-permute-start | bytes 4718600 | tf_op jit(solution)/shard_map/ppermute | solution.py:354
  262.7 1.6 copy-start

commit v3 on v2

--- a/solution.py
+++ b/solution.py
@@ -35,24 +35,41 @@
     return (head * cosine + other * sine).astype(BF16)
 
 
-def norm_kv_kernel(x_ref, gain_ref, wk_ref, wv_ref, cos_ref, sin_ref, h_ref, kv_ref, k_ref, v_ref):
-    x = x_ref[...].astype(F32)
-    width = x.shape[1]
-    mean = jnp.sum(x, axis=1, keepdims=True) * (1.0 / width)
-    centered = x - mean
-    var = jnp.sum(centered * centered, axis=1, keepdims=True) * (1.0 / width)
-    h_ref[...] = (centered * lax.rsqrt(var + LN_EPS) * gain_ref[...].astype(F32)[None, :]).astype(BF16)
-    k = jnp.dot(h_ref[...], wk_ref[...], preferred_element_type=F32).astype(BF16)
-    v = jnp.dot(h_ref[...], wv_ref[...], preferred_element_type=F32).astype(BF16)
-    v_ref[...] = v
-    cosine, sine = cos_ref[...], sin_ref[...]
-    for head in range(k.shape[1] // HEAD_DIM):
-        cols = slice(head * HEAD_DIM, (head + 1) * HEAD_DIM)
-        rotated = rotate_head(k[:, cols].astype(F32), cosine, sine)
-        k_ref[:, cols] = rotated
-        kv_ref[head, 0] = rotated
-        for start in range(0, k.shape[0], HEAD_DIM):
-            kv_ref[head, 1, start:start + HEAD_DIM, :] = v[start:start + HEAD_DIM, cols].T
+def norm_kv_kernel(x_ref, gain_ref, wk_ref, wv_ref, cos_ref, sin_ref, h_ref, kv_ref, k_ref, v_ref, even_ref, odd_ref):
+    step = pl.program_id(0)
+
+    def body(made, used):
+        k = jnp.dot(used[...], wk_ref[...], preferred_element_type=F32).astype(BF16)
+        v = jnp.dot(used[...], wv_ref[...], preferred_element_type=F32).astype(BF16)
+        x = x_ref[...].astype(F32)
+        width = x.shape[1]
+        mean = jnp.sum(x, axis=1, keepdims=True) * (1.0 / width)
+        centered = x - mean
+        var = jnp.sum(centered * centered, axis=1, keepdims=True) * (1.0 / width)
+        h = (centered * lax.rsqrt(var + LN_EPS) * gain_ref[...].astype(F32)[None, :]).astype(BF16)
+        made[...] = h
+        h_ref[...] = h
+        v_ref[...] = v
+        cosine, sine = cos_ref[...], sin_ref[...]
+        for head in range(k.shape[1] // HEAD_DIM):
+            cols = slice(head * HEAD_DIM, (head + 1) * HEAD_DIM)
+            rotated = rotate_head(k[:, cols].astype(F32), cosine, sine)
+            k_ref[:, cols] = rotated
+            kv_ref[head, 0] = rotated
+            for start in range(0, k.shape[0], HEAD_DIM):
+                kv_ref[head, 1, start:start + HEAD_DIM, :] = v[start:start + HEAD_DIM, cols].T
+
+    @pl.when(step == 0)
+    def _():
+        odd_ref[...] = jnp.zeros_like(odd_ref)
+
+    @pl.when(step % 2 == 0)
+    def _():
+        body(even_ref, odd_ref)
+
+    @pl.when(step % 2 == 1)
+    def _():
+        body(odd_ref, even_ref)
 
 
 def norm_kv(x, gain, wk, wv, cosine, sine):
@@ -60,22 +77,23 @@
     kv = wk.shape[1]
     groups = kv // HEAD_DIM
     tile = 256
+    tiles = rows // tile
     return pl.pallas_call(
         norm_kv_kernel,
-        grid=(rows // tile,),
+        grid=(tiles + 1,),
         in_specs=[
-            pl.BlockSpec((tile, width), lambda i: (i, 0)),
+            pl.BlockSpec((tile, width), lambda i: (jnp.minimum(i, tiles - 1), 0)),
             pl.BlockSpec((width,), lambda i: (0,)),
             pl.BlockSpec((width, kv), lambda i: (0, 0)),
             pl.BlockSpec((width, kv), lambda i: (0, 0)),
-            pl.BlockSpec((tile, HEAD_DIM), lambda i: (i, 0)),
-            pl.BlockSpec((tile, HEAD_DIM), lambda i: (i, 0)),
+            pl.BlockSpec((tile, HEAD_DIM), lambda i: (jnp.maximum(i - 1, 0), 0)),
+            pl.BlockSpec((tile, HEAD_DIM), lambda i: (jnp.maximum(i - 1, 0), 0)),
         ],
         out_specs=[
-            pl.BlockSpec((tile, width), lambda i: (i, 0)),
-            pl.BlockSpec((groups, 2, tile, HEAD_DIM), lambda i: (0, 0, i, 0)),
-            pl.BlockSpec((tile, kv), lambda i: (i, 0)),
-            pl.BlockSpec((tile, kv), lambda i: (i, 0)),
+            pl.BlockSpec((tile, width), lambda i: (jnp.minimum(i, tiles - 1), 0)),
+            pl.BlockSpec((groups, 2, tile, HEAD_DIM), lambda i: (0, 0, jnp.maximum(i - 1, 0), 0)),
+            pl.BlockSpec((tile, kv), lambda i: (jnp.maximum(i - 1, 0), 0)),
+            pl.BlockSpec((tile, kv), lambda i: (jnp.maximum(i - 1, 0), 0)),
         ],
         out_shape=[
             jax.ShapeDtypeStruct((rows, width), BF16),
@@ -83,6 +101,7 @@
             jax.ShapeDtypeStruct((rows, kv), BF16),
             jax.ShapeDtypeStruct((rows, kv), BF16),
         ],
+        scratch_shapes=[pltpu.VMEM((tile, width), BF16)] * 2,
         cost_estimate=cost(4 * rows * width * kv, 4 * rows * width + 4 * width * kv),
         name='norm_kv',
     )(x, gain, wk, wv, cosine, sine)
@@ -311,7 +330,8 @@
     ('down', 0, 512, 0, 3072),
     ('mlp', 512, 512, 0, 4096),
     ('own', 512, 512, 512),
-    ('down', 512, 512, 0, 1536),
+    ('down', 512, 512, 1024, 512),
+    ('down', 512, 512, 0, 1024),
     ('down', 512, 512, 1536, 1536),
 )
 

time: 301 us -> 331 us (1.100)
  waiting for transfers between devices: 53.8 us -> 73.4 us
  Pallas kernels: 227 us -> 238 us
    ppermute x3 -> x4, waiting for transfers between devices: 24 us -> 43.6 us  [local_layer(): other = lax.ppermute(last, 'tp', [(0, 1), (1, 0)])]
    pallas_call x3 -> x4, Pallas kernels: 53.6 us -> 58.8 us  [down(): pl.pallas_call(functools.partial(down_kernel, len(acts), len(attns), stre...]
    pallas_call x1, Pallas kernels: 15.6 us -> 19.1 us  [norm_kv(): pl.pallas_call(norm_kv_kernel, grid=(tiles + 1,), in_specs=[pl.BlockSpec(...]
    pallas_call x3 -> x4, Pallas kernels: 12.4 us -> 13.9 us  [add_chunk(): pl.pallas_call(add_kernel, grid=(rows // tile,), in_specs=specs, out_spec...]
  transfers between devices with their start and end apart: 6 -> 7, of which waited for: 3 -> 2; matrix products, arithmetic and copies ran while one was open for 2% -> 1% of each run, Pallas kernels for 51% -> 48%
where the time goes in v3:
time: 331 us
  Pallas kernels  238 us (72%)
  waiting for transfers between devices  73.4 us (22%)
  starting transfers between devices  9.12 us (3%)
  local copies, waits for them, and re-layouts  5.44 us (2%)
  other arithmetic  4.3 us (1%)
    pallas_call x2, Pallas kernels, gate_up(): pl.pallas_call(gate_up_kernel, grid=(cols // tile,), in_specs=[pl.BlockSp...  64.8 us
    pallas_call x2, Pallas kernels, attend(): pl.pallas_call(functools.partial(attend_kernel, base, tile, 512, group, b...  64.7 us
    pallas_call x4, Pallas kernels, down(): pl.pallas_call(functools.partial(down_kernel, len(acts), len(attns), stre...  58.8 us
    ppermute x4, waiting for transfers between devices, local_layer(): other = lax.ppermute(last, 'tp', [(0, 1), (1, 0)])  43.6 us
    ppermute x1, waiting for transfers between devices, local_layer(): kv_b = send(kv_own, perm=[(0, 2), (1, 3)])  29.8 us
    pallas_call x1, Pallas kernels, norm_kv(): pl.pallas_call(norm_kv_kernel, grid=(tiles + 1,), in_specs=[pl.BlockSpec(...  19.1 us
    pallas_call x1, Pallas kernels, q_proj(): pl.pallas_call(q_kernel, grid=(cols // tile,), in_specs=[pl.BlockSpec((ro...  16.2 us
    pallas_call x4, Pallas kernels, add_chunk(): pl.pallas_call(add_kernel, grid=(rows // tile,), in_specs=specs, out_spec...  13.9 us
  transfers between devices with their start and end apart: 7, of which 2 were waited for; matrix products, arithmetic and copies ran while one was open for 1% of the time, Pallas kernels for 48%

profile of v3, /device:TPU:3, one launch (start us, length us, event | category | flops | bytes accessed | tf_op | source)
XLA Modules:
  0.0 330.5 jit_solution(1182455085130504112)
XLA Ops:
  0.6 0.7 convert_element_type.10
  1.3 3.0 fusion
  4.4 19.1 %norm_kv.1 = (bf16[1024,3072]{1,0:T(8,128)(2,1)}, bf16[4,2,1024,128]{3,2,1,0:T(8,128)(2,1)}, bf16[1024,512]{1,0:T(8,128)(2,1)}, bf16[1024,512]{1,0:T(8,128)(2,1)}) custom-call(bf16[1024,3072]{1,0:T(8,128)(2,1)} %x_ref.9, bf16[3072]{0:T(1024)(128)(2,1)} %gain_ref.1, bf16[3072,512]{1,0:T(8,128)(2,1)} %wk_ref.1, bf16[3072,512]{1,0:T(8,128)(2,1)} %wv_ref.1, ...), custom_call_target="tpu_custom_call" | custom-call | flops 6442450944 | bytes 18874368 | tf_op jit(solution)/shard_map/norm_kv/pallas_call | solution.py:81
  23.5 1.3 collective-permute-start.1
  24.8 1.3 collective-permute-start
  26.1 16.2 %q_proj.1.q_ref = bf16[1024,1536]{1,0:T(8,128)(2,1)} custom-call(bf16[1024,3072]{1,0:T(8,128)(2,1)} %get-tuple-element.18.h_ref, bf16[3072,1536]{1,0:T(8,128)(2,1)} %w_ref.1, f32[1024,128]{1,0:T(8,128)} %get-tuple-element.26.cos_ref, f32[1024,128]{1,0:T(8,128)} %get-tuple-element.25.sin_ref), custom_call_target="tpu_custom_call" | custom-call | flops 9663676416 | bytes 15728640 | tf_op jit(solution)/shard_map/q_proj/pallas_call | solution.py:124
  42.3 29.8 %collective-permute-done.1.refs_2_ = bf16[4,2,1024,128]{3,2,1,0:T(8,128)(2,1)S(1)} collective-permute-done((bf16[4,2,1024,128]{3,2,1,0:T(8,128)(2,1)}, bf16[4,2,1024,128]{3,2,1,0:T(8,128)(2,1)S(1)}, u32[]{:S(2)}, u32[]{:S(2)}) %collective-permute-start.1) | collective-permute-done | bytes 2097184 | tf_op jit(solution)/shard_map/ppermute | solution.py:349
  72.1 0.0 copy-start.3
  72.1 3.6 %collective-permute-start.2 = (bf16[4,2,1024,128]{3,2,1,0:T(8,128)(2,1)S(1)}, bf16[4,2,1024,128]{3,2,1,0:T(8,128)(2,1)}, u32[]{:S(2)}, u32[]{:S(2)}) collective-permute-start(bf16[4,2,1024,128]{3,2,1,0:T(8,128)(2,1)S(1)} %collective-permute-done.1.refs_2_), channel_id=1, source_target_pairs={{2,3},{3,2},{6,7},{7,6}} | collective-permute-start | bytes 6291464 | tf_op jit(solution)/shard_map/ppermute | solution.py:351
  75.8 32.4 %gate_up.2.refs_0_ = bf16[512,4096]{1,0:T(8,128)(2,1)} custom-call(bf16[1024,3072]{1,0:T(8,128)(2,1)} %get-tuple-element.18.h_ref, bf16[3072,4096]{1,0:T(8,128)(2,1)} %wg_ref.3, bf16[3072,4096]{1,0:T(8,128)(2,1)} %wu_ref.3), custom_call_target="tpu_custom_call" | custom-call | flops 25769803776 | bytes 57671680 | tf_op jit(solution)/shard_map/gate_up/pallas_call | solution.py:250
  108.2 0.0 copy-done.3
  108.2 0.6 pad_add_fusion.flags_ref
  108.8 0.0 collective-permute-done.refs_1_
  108.8 0.0 collective-permute-done.2.refs_3_
  108.8 30.6 %attend.2.refs_1_ = bf16[512,1536]{1,0:T(8,128)(2,1)} custom-call(s32[2]{0:T(128)} %pad_add_fusion.flags_ref, bf16[1024,1536]{1,0:T(8,128)(2,1)} %q_proj.1.q_ref, bf16[4,2,1024,128]{3,2,1,0:T(8,128)(2,1)} %get-tuple-element.17.refs_0_, bf16[4,2,1024,128]{3,2,1,0:T(8,128)(2,1)} %collective-permute-done.refs_1_, bf16[4,2,1024,128]{3,2,1,0:T(8,128)(2,1)} %copy-done.3, ...), custom_call_target="tpu_custom_call" | custom-call | flops 8053063680 | bytes 8388608 | tf_op jit(solution)/shard_map/attend/pallas_call | solution.py:230
  139.4 24.2 %down.4.mine_ref = bf16[512,3072]{1,0:T(8,128)(2,1)} custom-call(bf16[512,4096]{1,0:T(8,128)(2,1)} %gate_up.2.refs_0_, bf16[512,1536]{1,0:T(8,128)(2,1)} %attend.2.refs_1_, bf16[4096,3072]{1,0:T(8,128)(2,1)} %refs_2_.7, bf16[1536,3072]{1,0:T(8,128)(2,1)} %refs_3_.7), custom_call_target="tpu_custom_call" | custom-call | flops 17716740096 | bytes 34603008 | tf_op jit(solution)/shard_map/down/pallas_call | solution.py:287
  163.6 1.2 collective-permute-start.6
  164.8 32.4 %gate_up.3.refs_0_ = bf16[512,4096]{1,0:T(8,128)(2,1)} custom-call(bf16[1024,3072]{1,0:T(8,128)(2,1)} %get-tuple-element.18.h_ref, bf16[3072,4096]{1,0:T(8,128)(2,1)} %wg_ref.3, bf16[3072,4096]{1,0:T(8,128)(2,1)} %wu_ref.3), custom_call_target="tpu_custom_call" | custom-call | flops 25769803776 | bytes 57671680 | tf_op jit(solution)/shard_map/gate_up/pallas_call | solution.py:250
  197.2 34.1 %attend.3.refs_1_ = bf16[512,1536]{1,0:T(8,128)(2,1)} custom-call(s32[2]{0:T(128)} %pad_add_fusion.flags_ref, bf16[1024,1536]{1,0:T(8,128)(2,1)} %q_proj.1.q_ref, bf16[4,2,1024,128]{3,2,1,0:T(8,128)(2,1)} %get-tuple-element.17.refs_0_, bf16[4,2,1024,128]{3,2,1,0:T(8,128)(2,1)} %collective-permute-done.refs_1_, bf16[4,2,1024,128]{3,2,1,0:T(8,128)(2,1)} %copy-done.3, ...), custom_call_target="tpu_custom_call" | custom-call | flops 8053063680 | bytes 8388608 | tf_op jit(solution)/shard_map/attend/pallas_call | solution.py:230
  231.3 8.3 %down.5.mine_ref = bf16[512,512]{1,0:T(8,128)(2,1)} custom-call(bf16[512,4096]{1,0:T(8,128)(2,1)} %gate_up.3.refs_0_, bf16[512,1536]{1,0:T(8,128)(2,1)} %attend.3.refs_1_, bf16[4096,3072]{1,0:T(8,128)(2,1)} %refs_2_.7, bf16[1536,3072]{1,0:T(8,128)(2,1)} %refs_3_.7), custom_call_target="tpu_custom_call" | custom-call | flops 2952790016 | bytes 5767168 | tf_op jit(solution)/shard_map/down/pallas_call | solution.py:287
  239.6 11.6 %down.6.mine_ref = bf16[512,1024]{1,0:T(8,128)(2,1)} custom-call(bf16[512,4096]{1,0:T(8,128)(2,1)} %gate_up.3.refs_0_, bf16[512,1536]{1,0:T(8,128)(2,1)} %attend.3.refs_1_, bf16[4096,3072]{1,0:T(8,128)(2,1)} %refs_2_.7, bf16[1536,3072]{1,0:T(8,128)(2,1)} %refs_3_.7), custom_call_target="tpu_custom_call" | custom-call | flops 5905580032 | bytes 11534336 | tf_op jit(solution)/shard_map/down/pallas_call | solution.py:287
  251.1 0.0 copy-start
  251.1 0.0 copy-start.1
  251.1 14.8 %down.7.mine_ref = bf16[512,1536]{1,0:T(8,128)(2,1)} custom-call(bf16[512,4096]{1,0:T(8,128)(2,1)} %gate_up.3.refs_0_, bf16[512,1536]{1,0:T(8,128)(2,1)} %attend.3.refs_1_, bf16[4096,3072]{1,0:T(8,128)(2,1)} %refs_2_.7, bf16[1536,3072]{1,0:T(8,128)(2,1)} %refs_3_.7), custom_call_target="tpu_custom_call" | custom-call | flops 8858370048 | bytes 17301504 | tf_op jit(solution)/shard_map/down/pallas_call | solution.py:287
  265.9 0.2 collective-permute-start.3
  266.1 0.0 copy-done
  266.1 1.2 collective-permute-start.4
  267.4 0.0 copy-done.1
  267.4 0.2 collective-permute-start.5
  267.6 2.1 reshape.42
  269.7 2.1 reshape.43
  271.9 0.0 collective-permute-done.6.other_ref
  271.9 5.5 %add.31.refs_0_ = bf16[1024,3072]{1,0:T(8,128)(2,1)} custom-call(bf16[1024,3072]{1,0:T(8,128)(2,1)} %x_ref.9, bf16[512,3072]{1,0:T(8,128)(2,1)} %down.4.mine_ref, bf16[512,3072]{1,0:T(8,128)(2,1)} %collective-permute-done.6.other_ref), custom_call_target="tpu_custom_call" | custom-call | flops 4718592 | bytes 12582912 | tf_op jit(solution)/shard_map/add/pallas_call | solution.py:315
  277.3 43.6 %collective-permute-done.5.other_ref = bf16[512,512]{1,0:T(8,128)(2,1)} collective-permute-done((bf16[512,512]{1,0:T(8,128)(2,1)S(1)}, bf16[512,512]{1,0:T(8,128)(2,1)}, u32[]{:S(2)}, u32[]{:S(2)}) %collective-permute-start.5) | collective-permute-done | bytes 524320 | tf_op jit(solution)/shard_map/ppermute | solution.py:374
  320.9 2.1 add.32.refs_0_
  323.1 0.0 collective-permute-done.4.other_ref
  323.1 2.8 add.33.refs_0_
  325.9 0.0 collective-permute-done.3.other_ref
  325.9 0.0 copy-start.2
  325.9 1.2 copy-done.2
  327.1 3.5 %add.34 = bf16[1024,3072]{1,0:T(8,128)(2,1)} custom-call(bf16[1024,3072]{1,0:T(8,128)(2,1)} %x_ref.9, bf16[512,1536]{1,0:T(8,128)(2,1)} %down.7.mine_ref, bf16[512,1536]{1,0:T(8,128)(2,1)} %copy-done.2, bf16[1024,3072]{1,0:T(8,128)(2,1)} %add.33.refs_0_), custom_call_target="tpu_custom_call", output_to_operand_aliasing={{}: (3, {})} | custom-call | flops 2359296 | bytes 6291456 | tf_op jit(solution)/shard_map/add/pallas_call | solution.py:315
  (1 shorter events, 0.0 us)
Async XLA Ops:
  23.5 48.6 %collective-permute-start.1 = (bf16[4,2,1024,128]{3,2,1,0:T(8,128)(2,1)}, bf16[4,2,1024,128]{3,2,1,0:T(8,128)(2,1)S(1)}, u32[]{:S(2)}, u32[]{:S(2)}) collective-permute-start(bf16[4,2,1024,128]{3,2,1,0:T(8,128)(2,1)} %get-tuple-element.17.refs_0_), channel_id=1, source_target_pairs={{0,2},{1,3},{4,6},{5,7}} | collective-permute-start | bytes 6291464 | tf_op jit(solution)/shard_map/ppermute | solution.py:349
  24.8 83.9 %collective-permute-start = (bf16[4,2,1024,128]{3,2,1,0:T(8,128)(2,1)}, bf16[4,2,1024,128]{3,2,1,0:T(8,128)(2,1)}, u32[]{:S(2)}, u32[]{:S(2)}) collective-permute-start(bf16[4,2,1024,128]{3,2,1,0:T(8,128)(2,1)} %get-tuple-element.17.refs_0_), channel_id=1, source_target_pairs={{0,1},{2,3},{4,5},{6,7}} | collective-permute-start | bytes 6291464 | tf_op jit(solution)/shard_map/ppermute | solution.py:350
  72.1 36.1 %copy-start.3 = (bf16[4,2,1024,128]{3,2,1,0:T(8,128)(2,1)}, bf16[4,2,1024,128]{3,2,1,0:T(8,128)(2,1)S(1)}, u32[]{:S(2)}) copy-start(bf16[4,2,1024,128]{3,2,1,0:T(8,128)(2,1)S(1)} %collective-permute-done.1.refs_2_) | copy-start | bytes 6291460
  72.1 36.6 %collective-permute-start.2 = (bf16[4,2,1024,128]{3,2,1,0:T(8,128)(2,1)S(1)}, bf16[4,2,1024,128]{3,2,1,0:T(8,128)(2,1)}, u32[]{:S(2)}, u32[]{:S(2)}) collective-permute-start(bf16[4,2,1024,128]{3,2,1,0:T(8,128)(2,1)S(1)} %collective-permute-done.1.refs_2_), channel_id=1, source_target_pairs={{2,3},{3,2},{6,7},{7,6}} | collective-permute-start | bytes 6291464 | tf_op jit(solution)/shard_map/ppermute | solution.py:351
  163.6 108.3 %collective-permute-start.6 = (bf16[512,3072]{1,0:T(8,128)(2,1)}, bf16[512,3072]{1,0:T(8,128)(2,1)}, u32[]{:S(2)}, u32[]{:S(2)}) collective-permute-start(bf16[512,3072]{1,0:T(8,128)(2,1)} %down.4.mine_ref), channel_id=1, source_target_pairs={{0,4},{4,0},{1,5},{5,1},{2,6},{6,2},{3,7},{7,3}} | collective-permute-start | bytes 9437192 | tf_op jit(solution)/shard_map/ppermute | solution.py:374
  251.1 15.0 %copy-start = (bf16[512,1024]{1,0:T(8,128)(2,1)S(1)}, bf16[512,1024]{1,0:T(8,128)(2,1)}, u32[]{:S(2)}) copy-start(bf16[512,1024]{1,0:T(8,128)(2,1)} %down.6.mine_ref) | copy-start | bytes 3145732
  251.1 16.3 %copy-start.1 = (bf16[512,512]{1,0:T(8,128)(2,1)S(1)}, bf16[512,512]{1,0:T(8,128)(2,1)}, u32[]{:S(2)}) copy-start(bf16[512,512]{1,0:T(8,128)(2,1)} %down.5.mine_ref) | copy-start | bytes 1572868
  265.9 60.0 %collective-permute-start.3 = (bf16[512,1536]{1,0:T(8,128)(2,1)}, bf16[512,1536]{1,0:T(8,128)(2,1)S(1)}, u32[]{:S(2)}, u32[]{:S(2)}) collective-permute-start(bf16[512,1536]{1,0:T(8,128)(2,1)} %down.7.mine_ref), channel_id=1, source_target_pairs={{0,4},{4,0},{1,5},{5,1},{2,6},{6,2},{3,7},{7,3}} | collective-permute-start | bytes 4718600 | tf_op jit(solution)/shard_map/ppermute | solution.py:374
  266.1 56.9 %collective-permute-start.4 = (bf16[512,1024]{1,0:T(8,128)(2,1)S(1)}, bf16[512,1024]{1,0:T(8,128)(2,1)}, u32[]{:S(2)}, u32[]{:S(2)}) collective-permute-start(bf16[512,1024]{1,0:T(8,128)(2,1)S(1)} %copy-done), channel_id=1, source_target_pairs={{0,4},{4,0},{1,5},{5,1},{2,6},{6,2},{3,7},{7,3}} | collective-permute-start | bytes 3145736 | tf_op jit(solution)/shard_map/ppermute | solution.py:374
  267.4 53.5 %collective-permute-start.5 = (bf16[512,512]{1,0:T(8,128)(2,1)S(1)}, bf16[512,512]{1,0:T(8,128)(2,1)}, u32[]{:S(2)}, u32[]{:S(2)}) collective-permute-start(bf16[512,512]{1,0:T(8,128)(2,1)S(1)} %copy-done.1), channel_id=1, source_target_pairs={{0,4},{4,0},{1,5},{5,1},{2,6},{6,2},{3,7},{7,3}} | collective-permute-start | bytes 1572872 | tf_op jit(solution)/shard_map/ppermute | solution.py:374
  325.9 1.2 copy-start.2

commit v4 on v2

--- a/solution.py
+++ b/solution.py
@@ -35,13 +35,26 @@
     return (head * cosine + other * sine).astype(BF16)
 
 
-def norm_kv_kernel(x_ref, gain_ref, wk_ref, wv_ref, cos_ref, sin_ref, h_ref, kv_ref, k_ref, v_ref):
+def norm_kv_kernel(x_ref, gain_ref, wk_hbm, wv_hbm, cos_ref, sin_ref, h_ref, kv_ref, k_ref, v_ref, wk_ref, wv_ref, sems):
+    copies = [pltpu.make_async_copy(wk_hbm, wk_ref, sems.at[0]), pltpu.make_async_copy(wv_hbm, wv_ref, sems.at[1])]
+
+    @pl.when(pl.program_id(0) == 0)
+    def _():
+        for copy in copies:
+            copy.start()
+
     x = x_ref[...].astype(F32)
     width = x.shape[1]
     mean = jnp.sum(x, axis=1, keepdims=True) * (1.0 / width)
     centered = x - mean
     var = jnp.sum(centered * centered, axis=1, keepdims=True) * (1.0 / width)
     h_ref[...] = (centered * lax.rsqrt(var + LN_EPS) * gain_ref[...].astype(F32)[None, :]).astype(BF16)
+
+    @pl.when(pl.program_id(0) == 0)
+    def _():
+        for copy in copies:
+            copy.wait()
+
     k = jnp.dot(h_ref[...], wk_ref[...], preferred_element_type=F32).astype(BF16)
     v = jnp.dot(h_ref[...], wv_ref[...], preferred_element_type=F32).astype(BF16)
     v_ref[...] = v
@@ -66,8 +79,8 @@
         in_specs=[
             pl.BlockSpec((tile, width), lambda i: (i, 0)),
             pl.BlockSpec((width,), lambda i: (0,)),
-            pl.BlockSpec((width, kv), lambda i: (0, 0)),
-            pl.BlockSpec((width, kv), lambda i: (0, 0)),
+            pl.BlockSpec(memory_space=pl.ANY),
+            pl.BlockSpec(memory_space=pl.ANY),
             pl.BlockSpec((tile, HEAD_DIM), lambda i: (i, 0)),
             pl.BlockSpec((tile, HEAD_DIM), lambda i: (i, 0)),
         ],
@@ -83,35 +96,34 @@
             jax.ShapeDtypeStruct((rows, kv), BF16),
             jax.ShapeDtypeStruct((rows, kv), BF16),
         ],
+        scratch_shapes=[pltpu.VMEM((width, kv), BF16), pltpu.VMEM((width, kv), BF16), pltpu.SemaphoreType.DMA((2,))],
         cost_estimate=cost(4 * rows * width * kv, 4 * rows * width + 4 * width * kv),
         name='norm_kv',
     )(x, gain, wk, wv, cosine, sine)
 
 
 def q_kernel(h_ref, w_ref, cos_ref, sin_ref, q_ref):
-    for start in range(0, h_ref.shape[0], 512):
-        rows = slice(start, start + 512)
-        q = jnp.dot(h_ref[rows, :], w_ref[...], preferred_element_type=F32).astype(BF16)
-        cosine, sine = cos_ref[rows, :], sin_ref[rows, :]
-        for head in range(q.shape[1] // HEAD_DIM):
-            cols = slice(head * HEAD_DIM, (head + 1) * HEAD_DIM)
-            q_ref[rows, cols] = rotate_head(q[:, cols].astype(F32), cosine, sine)
+    q = jnp.dot(h_ref[...], w_ref[...], preferred_element_type=F32).astype(BF16)
+    cosine, sine = cos_ref[...], sin_ref[...]
+    for head in range(q.shape[1] // HEAD_DIM):
+        cols = slice(head * HEAD_DIM, (head + 1) * HEAD_DIM)
+        q_ref[:, cols] = rotate_head(q[:, cols].astype(F32), cosine, sine)
 
 
 def q_proj(h, wq, cosine, sine):
     rows, width = h.shape
     cols = wq.shape[1]
-    tile = 512
+    tile, half = 512, 512
     return pl.pallas_call(
         q_kernel,
-        grid=(cols // tile,),
+        grid=(rows // half, cols // tile),
         in_specs=[
-            pl.BlockSpec((rows, width), lambda i: (0, 0)),
-            pl.BlockSpec((width, tile), lambda i: (0, i)),
-            pl.BlockSpec((rows, HEAD_DIM), lambda i: (0, 0)),
-            pl.BlockSpec((rows, HEAD_DIM), lambda i: (0, 0)),
-        ],
-        out_specs=pl.BlockSpec((rows, tile), lambda i: (0, i)),
+            pl.BlockSpec((half, width), lambda r, i: (r, 0)),
+            pl.BlockSpec((width, tile), lambda r, i: (0, i)),
+            pl.BlockSpec((half, HEAD_DIM), lambda r, i: (r, 0)),
+            pl.BlockSpec((half, HEAD_DIM), lambda r, i: (r, 0)),
+        ],
+        out_specs=pl.BlockSpec((half, tile), lambda r, i: (r, i)),
         out_shape=jax.ShapeDtypeStruct((rows, cols), BF16),
         cost_estimate=cost(2 * rows * width * cols, 2 * rows * width + 2 * width * cols),
         name='q_proj',
@@ -225,7 +237,7 @@
 
 def gate_up(h, wg, wu, first, rows, col, cols):
     width = wg.shape[0]
-    tile = 512
+    tile = 256 if first == 0 else 512
     index, start = first // rows, col // tile
     weight_spec = pl.BlockSpec((width, tile), lambda i: (0, start + i))
     return pl.pallas_call(
@@ -311,8 +323,9 @@
     ('down', 0, 512, 0, 3072),
     ('mlp', 512, 512, 0, 4096),
     ('own', 512, 512, 512),
-    ('down', 512, 512, 0, 1536),
+    ('down', 512, 512, 0, 1024),
     ('down', 512, 512, 1536, 1536),
+    ('down', 512, 512, 1024, 512),
 )
 
 

time: 301 us -> 317 us (1.053)
  Pallas kernels: 227 us -> 237 us
  waiting for transfers between devices: 53.8 us -> 58.6 us
    ppermute x3 -> x4, waiting for transfers between devices: 24 us -> 29.7 us  [local_layer(): other = lax.ppermute(last, 'tp', [(0, 1), (1, 0)])]
    pallas_call x3 -> x4, Pallas kernels: 53.6 us -> 58.8 us  [down(): pl.pallas_call(functools.partial(down_kernel, len(acts), len(attns), stre...]
    pallas_call x3 -> x4, Pallas kernels: 12.4 us -> 13.9 us  [add_chunk(): pl.pallas_call(add_kernel, grid=(rows // tile,), in_specs=specs, out_spec...]
  transfers between devices with their start and end apart: 6 -> 7, of which waited for: 3 -> 2; matrix products, arithmetic and copies ran while one was open for 2% -> 2% of each run, Pallas kernels for 51% -> 52%
where the time goes in v4:
time: 317 us; the launch traced here: 316 us
  Pallas kernels  237 us (75%)
  waiting for transfers between devices  58.6 us (18%)
  starting transfers between devices  9.13 us (3%)
  local copies, waits for them, and re-layouts  6.23 us (2%)
  other arithmetic  4.3 us (1%)
    pallas_call x2, Pallas kernels, gate_up(): pl.pallas_call(gate_up_kernel, grid=(cols // tile,), in_specs=[pl.BlockSp...  66.5 us
    pallas_call x2, Pallas kernels, attend(): pl.pallas_call(functools.partial(attend_kernel, base, tile, 512, group, b...  64.7 us
    pallas_call x4, Pallas kernels, down(): pl.pallas_call(functools.partial(down_kernel, len(acts), len(attns), stre...  58.8 us
    ppermute x4, waiting for transfers between devices, local_layer(): other = lax.ppermute(last, 'tp', [(0, 1), (1, 0)])  29.7 us
    ppermute x1, waiting for transfers between devices, local_layer(): kv_b = send(kv_own, perm=[(0, 2), (1, 3)])  28.8 us
    pallas_call x1, Pallas kernels, q_proj(): pl.pallas_call(q_kernel, grid=(rows // half, cols // tile), in_specs=[pl....  17.2 us
    pallas_call x1, Pallas kernels, norm_kv(): pl.pallas_call(norm_kv_kernel, grid=(rows // tile,), in_specs=[pl.BlockSp...  16.3 us
    pallas_call x4, Pallas kernels, add_chunk(): pl.pallas_call(add_kernel, grid=(rows // tile,), in_specs=specs, out_spec...  13.9 us
  transfers between devices with their start and end apart: 7, of which 2 were waited for; matrix products, arithmetic and copies ran while one was open for 2% of the time, Pallas kernels for 52%

profile of v4, /device:TPU:3, one launch (start us, length us, event | category | flops | bytes accessed | tf_op | source)
XLA Modules:
  0.0 316.3 jit_solution(11328677384995117739)
XLA Ops:
  0.6 0.7 convert_element_type.10
  1.3 3.0 fusion
  4.4 16.3 %norm_kv.1 = (bf16[1024,3072]{1,0:T(8,128)(2,1)}, bf16[4,2,1024,128]{3,2,1,0:T(8,128)(2,1)}, bf16[1024,512]{1,0:T(8,128)(2,1)}, bf16[1024,512]{1,0:T(8,128)(2,1)}) custom-call(bf16[1024,3072]{1,0:T(8,128)(2,1)} %x_ref.9, bf16[3072]{0:T(1024)(128)(2,1)} %gain_ref.1, bf16[3072,512]{1,0:T(8,128)(2,1)} %wk_hbm.1, bf16[3072,512]{1,0:T(8,128)(2,1)} %wv_hbm.1, ...), custom_call_target="tpu_custom_call" | custom-call | flops 6442450944 | bytes 18874368 | tf_op jit(solution)/shard_map/norm_kv/pallas_call | solution.py:76
  20.7 1.3 collective-permute-start.1
  22.0 1.3 collective-permute-start
  23.3 17.2 %q_proj.1.q_ref = bf16[1024,1536]{1,0:T(8,128)(2,1)} custom-call(bf16[1024,3072]{1,0:T(8,128)(2,1)} %get-tuple-element.18.h_ref, bf16[3072,1536]{1,0:T(8,128)(2,1)} %w_ref.1, f32[1024,128]{1,0:T(8,128)} %get-tuple-element.26.cos_ref, f32[1024,128]{1,0:T(8,128)} %get-tuple-element.25.sin_ref), custom_call_target="tpu_custom_call" | custom-call | flops 9663676416 | bytes 15728640 | tf_op jit(solution)/shard_map/q_proj/pallas_call | solution.py:117
  40.5 28.8 %collective-permute-done.1.refs_2_ = bf16[4,2,1024,128]{3,2,1,0:T(8,128)(2,1)S(1)} collective-permute-done((bf16[4,2,1024,128]{3,2,1,0:T(8,128)(2,1)}, bf16[4,2,1024,128]{3,2,1,0:T(8,128)(2,1)S(1)}, u32[]{:S(2)}, u32[]{:S(2)}) %collective-permute-start.1) | collective-permute-done | bytes 2097184 | tf_op jit(solution)/shard_map/ppermute | solution.py:342
  69.3 0.0 copy-start.3
  69.3 3.6 %collective-permute-start.2 = (bf16[4,2,1024,128]{3,2,1,0:T(8,128)(2,1)S(1)}, bf16[4,2,1024,128]{3,2,1,0:T(8,128)(2,1)}, u32[]{:S(2)}, u32[]{:S(2)}) collective-permute-start(bf16[4,2,1024,128]{3,2,1,0:T(8,128)(2,1)S(1)} %collective-permute-done.1.refs_2_), channel_id=1, source_target_pairs={{2,3},{3,2},{6,7},{7,6}} | collective-permute-start | bytes 6291464 | tf_op jit(solution)/shard_map/ppermute | solution.py:344
  72.9 34.1 %gate_up.2.refs_0_ = bf16[512,4096]{1,0:T(8,128)(2,1)} custom-call(bf16[1024,3072]{1,0:T(8,128)(2,1)} %get-tuple-element.18.h_ref, bf16[3072,4096]{1,0:T(8,128)(2,1)} %wg_ref.3, bf16[3072,4096]{1,0:T(8,128)(2,1)} %wu_ref.3), custom_call_target="tpu_custom_call" | custom-call | flops 25769803776 | bytes 57671680 | tf_op jit(solution)/shard_map/gate_up/pallas_call | solution.py:243
  107.1 0.0 copy-done.3
  107.1 0.6 pad_add_fusion.flags_ref
  107.6 0.0 collective-permute-done.refs_1_
  107.6 0.0 collective-permute-done.2.refs_3_
  107.6 30.6 %attend.2.refs_1_ = bf16[512,1536]{1,0:T(8,128)(2,1)} custom-call(s32[2]{0:T(128)} %pad_add_fusion.flags_ref, bf16[1024,1536]{1,0:T(8,128)(2,1)} %q_proj.1.q_ref, bf16[4,2,1024,128]{3,2,1,0:T(8,128)(2,1)} %get-tuple-element.17.refs_0_, bf16[4,2,1024,128]{3,2,1,0:T(8,128)(2,1)} %collective-permute-done.refs_1_, bf16[4,2,1024,128]{3,2,1,0:T(8,128)(2,1)} %copy-done.3, ...), custom_call_target="tpu_custom_call" | custom-call | flops 8053063680 | bytes 8388608 | tf_op jit(solution)/shard_map/attend/pallas_call | solution.py:223
  138.2 24.2 %down.4.mine_ref = bf16[512,3072]{1,0:T(8,128)(2,1)} custom-call(bf16[512,4096]{1,0:T(8,128)(2,1)} %gate_up.2.refs_0_, bf16[512,1536]{1,0:T(8,128)(2,1)} %attend.2.refs_1_, bf16[4096,3072]{1,0:T(8,128)(2,1)} %refs_2_.7, bf16[1536,3072]{1,0:T(8,128)(2,1)} %refs_3_.7), custom_call_target="tpu_custom_call" | custom-call | flops 17716740096 | bytes 34603008 | tf_op jit(solution)/shard_map/down/pallas_call | solution.py:280
  162.5 1.2 collective-permute-start.6
  163.7 32.4 %gate_up.3.refs_0_ = bf16[512,4096]{1,0:T(8,128)(2,1)} custom-call(bf16[1024,3072]{1,0:T(8,128)(2,1)} %get-tuple-element.18.h_ref, bf16[3072,4096]{1,0:T(8,128)(2,1)} %wg_ref.3, bf16[3072,4096]{1,0:T(8,128)(2,1)} %wu_ref.3), custom_call_target="tpu_custom_call" | custom-call | flops 25769803776 | bytes 57671680 | tf_op jit(solution)/shard_map/gate_up/pallas_call | solution.py:243
  196.1 34.1 %attend.3.refs_1_ = bf16[512,1536]{1,0:T(8,128)(2,1)} custom-call(s32[2]{0:T(128)} %pad_add_fusion.flags_ref, bf16[1024,1536]{1,0:T(8,128)(2,1)} %q_proj.1.q_ref, bf16[4,2,1024,128]{3,2,1,0:T(8,128)(2,1)} %get-tuple-element.17.refs_0_, bf16[4,2,1024,128]{3,2,1,0:T(8,128)(2,1)} %collective-permute-done.refs_1_, bf16[4,2,1024,128]{3,2,1,0:T(8,128)(2,1)} %copy-done.3, ...), custom_call_target="tpu_custom_call" | custom-call | flops 8053063680 | bytes 8388608 | tf_op jit(solution)/shard_map/attend/pallas_call | solution.py:223
  230.2 11.6 %down.5.mine_ref = bf16[512,1024]{1,0:T(8,128)(2,1)} custom-call(bf16[512,4096]{1,0:T(8,128)(2,1)} %gate_up.3.refs_0_, bf16[512,1536]{1,0:T(8,128)(2,1)} %attend.3.refs_1_, bf16[4096,3072]{1,0:T(8,128)(2,1)} %refs_2_.7, bf16[1536,3072]{1,0:T(8,128)(2,1)} %refs_3_.7), custom_call_target="tpu_custom_call" | custom-call | flops 5905580032 | bytes 11534336 | tf_op jit(solution)/shard_map/down/pallas_call | solution.py:280
  241.7 0.0 copy-start
  241.7 14.8 %down.6.mine_ref = bf16[512,1536]{1,0:T(8,128)(2,1)} custom-call(bf16[512,4096]{1,0:T(8,128)(2,1)} %gate_up.3.refs_0_, bf16[512,1536]{1,0:T(8,128)(2,1)} %attend.3.refs_1_, bf16[4096,3072]{1,0:T(8,128)(2,1)} %refs_2_.7, bf16[1536,3072]{1,0:T(8,128)(2,1)} %refs_3_.7), custom_call_target="tpu_custom_call" | custom-call | flops 8858370048 | bytes 17301504 | tf_op jit(solution)/shard_map/down/pallas_call | solution.py:280
  256.5 0.2 collective-permute-start.4
  256.7 0.0 copy-done
  256.7 1.2 collective-permute-start.5
  258.0 8.3 %down.7.mine_ref = bf16[512,512]{1,0:T(8,128)(2,1)} custom-call(bf16[512,4096]{1,0:T(8,128)(2,1)} %gate_up.3.refs_0_, bf16[512,1536]{1,0:T(8,128)(2,1)} %attend.3.refs_1_, bf16[4096,3072]{1,0:T(8,128)(2,1)} %refs_2_.7, bf16[1536,3072]{1,0:T(8,128)(2,1)} %refs_3_.7), custom_call_target="tpu_custom_call" | custom-call | flops 2952790016 | bytes 5767168 | tf_op jit(solution)/shard_map/down/pallas_call | solution.py:280
  266.2 0.2 collective-permute-start.3
  266.4 2.1 reshape.42
  268.6 2.1 reshape.43
  270.7 0.0 collective-permute-done.6.other_ref
  270.7 5.5 %add.31.refs_0_ = bf16[1024,3072]{1,0:T(8,128)(2,1)} custom-call(bf16[1024,3072]{1,0:T(8,128)(2,1)} %x_ref.9, bf16[512,3072]{1,0:T(8,128)(2,1)} %down.4.mine_ref, bf16[512,3072]{1,0:T(8,128)(2,1)} %collective-permute-done.6.other_ref), custom_call_target="tpu_custom_call" | custom-call | flops 4718592 | bytes 12582912 | tf_op jit(solution)/shard_map/add/pallas_call | solution.py:308
  276.2 29.7 %collective-permute-done.5.other_ref = bf16[512,1024]{1,0:T(8,128)(2,1)} collective-permute-done((bf16[512,1024]{1,0:T(8,128)(2,1)S(1)}, bf16[512,1024]{1,0:T(8,128)(2,1)}, u32[]{:S(2)}, u32[]{:S(2)}) %collective-permute-start.5) | collective-permute-done | bytes 1048608 | tf_op jit(solution)/shard_map/ppermute | solution.py:367
  305.9 2.8 add.32.refs_0_
  308.7 0.0 collective-permute-done.4.other_ref
  308.7 0.0 copy-start.1
  308.7 1.2 copy-done.1
  309.9 3.5 %add.33.refs_0_ = bf16[1024,3072]{1,0:T(8,128)(2,1)} custom-call(bf16[1024,3072]{1,0:T(8,128)(2,1)} %x_ref.9, bf16[512,1536]{1,0:T(8,128)(2,1)} %down.6.mine_ref, bf16[512,1536]{1,0:T(8,128)(2,1)} %copy-done.1, bf16[1024,3072]{1,0:T(8,128)(2,1)} %add.32.refs_0_), custom_call_target="tpu_custom_call", output_to_operand_aliasing={{}: (3, {})} | custom-call | flops 2359296 | bytes 6291456 | tf_op jit(solution)/shard_map/add/pallas_call | solution.py:308
  313.3 0.0 collective-permute-done.3.other_ref
  313.3 0.0 copy-start.2
  313.3 0.8 copy-done.2
  314.1 2.1 add.34
  (1 shorter events, 0.0 us)
Async XLA Ops:
  20.7 48.6 %collective-permute-start.1 = (bf16[4,2,1024,128]{3,2,1,0:T(8,128)(2,1)}, bf16[4,2,1024,128]{3,2,1,0:T(8,128)(2,1)S(1)}, u32[]{:S(2)}, u32[]{:S(2)}) collective-permute-start(bf16[4,2,1024,128]{3,2,1,0:T(8,128)(2,1)} %get-tuple-element.17.refs_0_), channel_id=1, source_target_pairs={{0,2},{1,3},{4,6},{5,7}} | collective-permute-start | bytes 6291464 | tf_op jit(solution)/shard_map/ppermute | solution.py:342
  22.0 85.6 %collective-permute-start = (bf16[4,2,1024,128]{3,2,1,0:T(8,128)(2,1)}, bf16[4,2,1024,128]{3,2,1,0:T(8,128)(2,1)}, u32[]{:S(2)}, u32[]{:S(2)}) collective-permute-start(bf16[4,2,1024,128]{3,2,1,0:T(8,128)(2,1)} %get-tuple-element.17.refs_0_), channel_id=1, source_target_pairs={{0,1},{2,3},{4,5},{6,7}} | collective-permute-start | bytes 6291464 | tf_op jit(solution)/shard_map/ppermute | solution.py:343
  69.3 37.8 %copy-start.3 = (bf16[4,2,1024,128]{3,2,1,0:T(8,128)(2,1)}, bf16[4,2,1024,128]{3,2,1,0:T(8,128)(2,1)S(1)}, u32[]{:S(2)}) copy-start(bf16[4,2,1024,128]{3,2,1,0:T(8,128)(2,1)S(1)} %collective-permute-done.1.refs_2_) | copy-start | bytes 6291460
  69.3 38.3 %collective-permute-start.2 = (bf16[4,2,1024,128]{3,2,1,0:T(8,128)(2,1)S(1)}, bf16[4,2,1024,128]{3,2,1,0:T(8,128)(2,1)}, u32[]{:S(2)}, u32[]{:S(2)}) collective-permute-start(bf16[4,2,1024,128]{3,2,1,0:T(8,128)(2,1)S(1)} %collective-permute-done.1.refs_2_), channel_id=1, source_target_pairs={{2,3},{3,2},{6,7},{7,6}} | collective-permute-start | bytes 6291464 | tf_op jit(solution)/shard_map/ppermute | solution.py:344
  162.5 108.2 %collective-permute-start.6 = (bf16[512,3072]{1,0:T(8,128)(2,1)}, bf16[512,3072]{1,0:T(8,128)(2,1)}, u32[]{:S(2)}, u32[]{:S(2)}) collective-permute-start(bf16[512,3072]{1,0:T(8,128)(2,1)} %down.4.mine_ref), channel_id=1, source_target_pairs={{0,4},{4,0},{1,5},{5,1},{2,6},{6,2},{3,7},{7,3}} | collective-permute-start | bytes 9437192 | tf_op jit(solution)/shard_map/ppermute | solution.py:367
  241.7 15.0 %copy-start = (bf16[512,1024]{1,0:T(8,128)(2,1)S(1)}, bf16[512,1024]{1,0:T(8,128)(2,1)}, u32[]{:S(2)}) copy-start(bf16[512,1024]{1,0:T(8,128)(2,1)} %down.5.mine_ref) | copy-start | bytes 3145732
  256.5 52.2 %collective-permute-start.4 = (bf16[512,1536]{1,0:T(8,128)(2,1)}, bf16[512,1536]{1,0:T(8,128)(2,1)S(1)}, u32[]{:S(2)}, u32[]{:S(2)}) collective-permute-start(bf16[512,1536]{1,0:T(8,128)(2,1)} %down.6.mine_ref), channel_id=1, source_target_pairs={{0,4},{4,0},{1,5},{5,1},{2,6},{6,2},{3,7},{7,3}} | collective-permute-start | bytes 4718600 | tf_op jit(solution)/shard_map/ppermute | solution.py:367
  256.7 49.2 %collective-permute-start.5 = (bf16[512,1024]{1,0:T(8,128)(2,1)S(1)}, bf16[512,1024]{1,0:T(8,128)(2,1)}, u32[]{:S(2)}, u32[]{:S(2)}) collective-permute-start(bf16[512,1024]{1,0:T(8,128)(2,1)S(1)} %copy-done), channel_id=1, source_target_pairs={{0,4},{4,0},{1,5},{5,1},{2,6},{6,2},{3,7},{7,3}} | collective-permute-start | bytes 3145736 | tf_op jit(solution)/shard_map/ppermute | solution.py:367
  266.2 47.1 %collective-permute-start.3 = (bf16[512,512]{1,0:T(8,128)(2,1)}, bf16[512,512]{1,0:T(8,128)(2,1)S(1)}, u32[]{:S(2)}, u32[]{:S(2)}) collective-permute-start(bf16[512,512]{1,0:T(8,128)(2,1)} %down.7.mine_ref), channel_id=1, source_target_pairs={{0,4},{4,0},{1,5},{5,1},{2,6},{6,2},{3,7},{7,3}} | collective-permute-start | bytes 1572872 | tf_op jit(solution)/shard_map/ppermute | solution.py:367
  308.7 1.2 copy-start.1
  313.3 0.8 copy-start.2

commit v5 on v2

--- a/solution.py
+++ b/solution.py
@@ -308,11 +308,14 @@
 SCHEDULE = (
     ('mlp', 0, 512, 0, 4096),
     ('own', 0, 512, 512),
-    ('down', 0, 512, 0, 3072),
+    ('down', 0, 512, 2560, 512),
+    ('down', 0, 512, 0, 2560),
     ('mlp', 512, 512, 0, 4096),
-    ('own', 512, 512, 512),
-    ('down', 512, 512, 0, 1536),
-    ('down', 512, 512, 1536, 1536),
+    ('own', 512, 256, 256),
+    ('down', 512, 256, 0, 3072),
+    ('own', 768, 256, 256),
+    ('down', 768, 256, 0, 1536),
+    ('down', 768, 256, 1536, 1536),
 )
 
 

time: 301 us -> 323 us (1.073)
  Pallas kernels: 227 us -> 251 us
    pallas_call x3 -> x5, Pallas kernels: 53.6 us -> 67.2 us  [down(): pl.pallas_call(functools.partial(down_kernel, len(acts), len(attns), stre...]
    pallas_call x2 -> x3, Pallas kernels: 64.7 us -> 70.4 us  [attend(): pl.pallas_call(functools.partial(attend_kernel, base, tile, 512, group, b...]
    pallas_call x3 -> x5, Pallas kernels: 12.4 us -> 16.5 us  [add_chunk(): pl.pallas_call(add_kernel, grid=(rows // tile,), in_specs=specs, out_spec...]
    ppermute x3 -> x5, waiting for transfers between devices: 24 us -> 21.3 us  [local_layer(): other = lax.ppermute(last, 'tp', [(0, 1), (1, 0)])]
  transfers between devices with their start and end apart: 6 -> 8, of which waited for: 3 -> 2; matrix products, arithmetic and copies ran while one was open for 2% -> 1% of each run, Pallas kernels for 51% -> 53%
where the time goes in v5:
time: 323 us
  Pallas kernels  251 us (78%)
  waiting for transfers between devices  51.1 us (16%)
  starting transfers between devices  10.3 us (3%)
  local copies, waits for them, and re-layouts  5.78 us (2%)
  other arithmetic  4.3 us (1%)
    pallas_call x3, Pallas kernels, attend(): pl.pallas_call(functools.partial(attend_kernel, base, tile, 512, group, b...  70.4 us
    pallas_call x5, Pallas kernels, down(): pl.pallas_call(functools.partial(down_kernel, len(acts), len(attns), stre...  67.2 us
    pallas_call x2, Pallas kernels, gate_up(): pl.pallas_call(gate_up_kernel, grid=(cols // tile,), in_specs=[pl.BlockSp...  64.8 us
    ppermute x1, waiting for transfers between devices, local_layer(): kv_b = send(kv_own, perm=[(0, 2), (1, 3)])  29.8 us
    ppermute x5, waiting for transfers between devices, local_layer(): other = lax.ppermute(last, 'tp', [(0, 1), (1, 0)])  21.3 us
    pallas_call x5, Pallas kernels, add_chunk(): pl.pallas_call(add_kernel, grid=(rows // tile,), in_specs=specs, out_spec...  16.5 us
    pallas_call x1, Pallas kernels, q_proj(): pl.pallas_call(q_kernel, grid=(cols // tile,), in_specs=[pl.BlockSpec((ro...  16.2 us
    pallas_call x1, Pallas kernels, norm_kv(): pl.pallas_call(norm_kv_kernel, grid=(rows // tile,), in_specs=[pl.BlockSp...  15.6 us
  transfers between devices with their start and end apart: 8, of which 2 were waited for; matrix products, arithmetic and copies ran while one was open for 1% of the time, Pallas kernels for 53%

profile of v5, /device:TPU:3, one launch (start us, length us, event | category | flops | bytes accessed | tf_op | source)
XLA Modules:
  0.0 322.9 jit_solution(8867866209287871381)
XLA Ops:
  0.6 0.7 convert_element_type.10
  1.3 3.0 fusion
  4.4 15.6 %norm_kv.1 = (bf16[1024,3072]{1,0:T(8,128)(2,1)}, bf16[4,2,1024,128]{3,2,1,0:T(8,128)(2,1)}, bf16[1024,512]{1,0:T(8,128)(2,1)}, bf16[1024,512]{1,0:T(8,128)(2,1)}) custom-call(bf16[1024,3072]{1,0:T(8,128)(2,1)} %x_ref.11, bf16[3072]{0:T(1024)(128)(2,1)} %gain_ref.1, bf16[3072,512]{1,0:T(8,128)(2,1)} %wk_ref.1, bf16[3072,512]{1,0:T(8,128)(2,1)} %wv_ref.1, ...), custom_call_target="tpu_custom_call" | custom-call | flops 6442450944 | bytes 18874368 | tf_op jit(solution)/shard_map/norm_kv/pallas_call | solution.py:63
  19.9 1.3 collective-permute-start.1
  21.2 1.3 collective-permute-start
  22.5 16.2 %q_proj.1.q_ref = bf16[1024,1536]{1,0:T(8,128)(2,1)} custom-call(bf16[1024,3072]{1,0:T(8,128)(2,1)} %get-tuple-element.22.h_ref, bf16[3072,1536]{1,0:T(8,128)(2,1)} %w_ref.1, f32[1024,128]{1,0:T(8,128)} %get-tuple-element.30.cos_ref, f32[1024,128]{1,0:T(8,128)} %get-tuple-element.29.sin_ref), custom_call_target="tpu_custom_call" | custom-call | flops 9663676416 | bytes 15728640 | tf_op jit(solution)/shard_map/q_proj/pallas_call | solution.py:105
  38.7 29.8 %collective-permute-done.1.refs_2_ = bf16[4,2,1024,128]{3,2,1,0:T(8,128)(2,1)S(1)} collective-permute-done((bf16[4,2,1024,128]{3,2,1,0:T(8,128)(2,1)}, bf16[4,2,1024,128]{3,2,1,0:T(8,128)(2,1)S(1)}, u32[]{:S(2)}, u32[]{:S(2)}) %collective-permute-start.1) | collective-permute-done | bytes 2097184 | tf_op jit(solution)/shard_map/ppermute | solution.py:332
  68.5 0.0 copy-start.2
  68.5 3.6 %collective-permute-start.2 = (bf16[4,2,1024,128]{3,2,1,0:T(8,128)(2,1)S(1)}, bf16[4,2,1024,128]{3,2,1,0:T(8,128)(2,1)}, u32[]{:S(2)}, u32[]{:S(2)}) collective-permute-start(bf16[4,2,1024,128]{3,2,1,0:T(8,128)(2,1)S(1)} %collective-permute-done.1.refs_2_), channel_id=1, source_target_pairs={{2,3},{3,2},{6,7},{7,6}} | collective-permute-start | bytes 6291464 | tf_op jit(solution)/shard_map/ppermute | solution.py:334
  72.2 32.4 %gate_up.2.refs_0_ = bf16[512,4096]{1,0:T(8,128)(2,1)} custom-call(bf16[1024,3072]{1,0:T(8,128)(2,1)} %get-tuple-element.22.h_ref, bf16[3072,4096]{1,0:T(8,128)(2,1)} %wg_ref.3, bf16[3072,4096]{1,0:T(8,128)(2,1)} %wu_ref.3), custom_call_target="tpu_custom_call" | custom-call | flops 25769803776 | bytes 57671680 | tf_op jit(solution)/shard_map/gate_up/pallas_call | solution.py:231
  104.6 0.0 copy-done.2
  104.6 0.6 pad_add_fusion.flags_ref
  105.2 0.0 collective-permute-done.refs_1_
  105.2 0.0 collective-permute-done.2.refs_3_
  105.2 30.6 %attend.3.refs_1_ = bf16[512,1536]{1,0:T(8,128)(2,1)} custom-call(s32[2]{0:T(128)} %pad_add_fusion.flags_ref, bf16[1024,1536]{1,0:T(8,128)(2,1)} %q_proj.1.q_ref, bf16[4,2,1024,128]{3,2,1,0:T(8,128)(2,1)} %get-tuple-element.19.refs_0_, bf16[4,2,1024,128]{3,2,1,0:T(8,128)(2,1)} %collective-permute-done.refs_1_, bf16[4,2,1024,128]{3,2,1,0:T(8,128)(2,1)} %copy-done.2, ...), custom_call_target="tpu_custom_call" | custom-call | flops 8053063680 | bytes 8388608 | tf_op jit(solution)/shard_map/attend/pallas_call | solution.py:211
  135.8 8.3 %down.5.mine_ref = bf16[512,512]{1,0:T(8,128)(2,1)} custom-call(bf16[512,4096]{1,0:T(8,128)(2,1)} %gate_up.2.refs_0_, bf16[512,1536]{1,0:T(8,128)(2,1)} %attend.3.refs_1_, bf16[4096,3072]{1,0:T(8,128)(2,1)} %refs_2_.9, bf16[1536,3072]{1,0:T(8,128)(2,1)} %refs_3_.9), custom_call_target="tpu_custom_call" | custom-call | flops 2952790016 | bytes 5767168 | tf_op jit(solution)/shard_map/down/pallas_call | solution.py:268
  144.1 21.0 %down.6.mine_ref = bf16[512,2560]{1,0:T(8,128)(2,1)} custom-call(bf16[512,4096]{1,0:T(8,128)(2,1)} %gate_up.2.refs_0_, bf16[512,1536]{1,0:T(8,128)(2,1)} %attend.3.refs_1_, bf16[4096,3072]{1,0:T(8,128)(2,1)} %refs_2_.9, bf16[1536,3072]{1,0:T(8,128)(2,1)} %refs_3_.9), custom_call_target="tpu_custom_call" | custom-call | flops 14763950080 | bytes 28835840 | tf_op jit(solution)/shard_map/down/pallas_call | solution.py:268
  165.2 1.2 collective-permute-start.6
  166.4 32.4 %gate_up.3.refs_0_ = bf16[512,4096]{1,0:T(8,128)(2,1)} custom-call(bf16[1024,3072]{1,0:T(8,128)(2,1)} %get-tuple-element.22.h_ref, bf16[3072,4096]{1,0:T(8,128)(2,1)} %wg_ref.3, bf16[3072,4096]{1,0:T(8,128)(2,1)} %wu_ref.3), custom_call_target="tpu_custom_call" | custom-call | flops 25769803776 | bytes 57671680 | tf_op jit(solution)/shard_map/gate_up/pallas_call | solution.py:231
  198.8 19.5 %attend.4.refs_1_ = bf16[256,1536]{1,0:T(8,128)(2,1)} custom-call(s32[2]{0:T(128)} %pad_add_fusion.flags_ref, bf16[1024,1536]{1,0:T(8,128)(2,1)} %q_proj.1.q_ref, bf16[4,2,1024,128]{3,2,1,0:T(8,128)(2,1)} %get-tuple-element.19.refs_0_, bf16[4,2,1024,128]{3,2,1,0:T(8,128)(2,1)} %collective-permute-done.refs_1_, bf16[4,2,1024,128]{3,2,1,0:T(8,128)(2,1)} %copy-done.2, ...), custom_call_target="tpu_custom_call" | custom-call | flops 4026531840 | bytes 8388608 | tf_op jit(solution)/shard_map/attend/pallas_call | solution.py:211
  218.3 17.0 %down.7.mine_ref = bf16[256,3072]{1,0:T(8,128)(2,1)} custom-call(bf16[512,4096]{1,0:T(8,128)(2,1)} %gate_up.3.refs_0_, bf16[256,1536]{1,0:T(8,128)(2,1)} %attend.4.refs_1_, bf16[4096,3072]{1,0:T(8,128)(2,1)} %refs_2_.9, bf16[1536,3072]{1,0:T(8,128)(2,1)} %refs_3_.9), custom_call_target="tpu_custom_call" | custom-call | flops 8858370048 | bytes 34603008 | tf_op jit(solution)/shard_map/down/pallas_call | solution.py:268
  235.3 0.2 collective-permute-start.5
  235.6 20.3 %attend.5.refs_1_ = bf16[256,1536]{1,0:T(8,128)(2,1)} custom-call(s32[2]{0:T(128)} %pad_add_fusion.flags_ref, bf16[1024,1536]{1,0:T(8,128)(2,1)} %q_proj.1.q_ref, bf16[4,2,1024,128]{3,2,1,0:T(8,128)(2,1)} %get-tuple-element.19.refs_0_, bf16[4,2,1024,128]{3,2,1,0:T(8,128)(2,1)} %collective-permute-done.refs_1_, bf16[4,2,1024,128]{3,2,1,0:T(8,128)(2,1)} %copy-done.2, ...), custom_call_target="tpu_custom_call" | custom-call | flops 4026531840 | bytes 8388608 | tf_op jit(solution)/shard_map/attend/pallas_call | solution.py:211
  255.8 10.4 %down.8.mine_ref = bf16[256,1536]{1,0:T(8,128)(2,1)} custom-call(bf16[512,4096]{1,0:T(8,128)(2,1)} %gate_up.3.refs_0_, bf16[256,1536]{1,0:T(8,128)(2,1)} %attend.5.refs_1_, bf16[4096,3072]{1,0:T(8,128)(2,1)} %refs_2_.9, bf16[1536,3072]{1,0:T(8,128)(2,1)} %refs_3_.9), custom_call_target="tpu_custom_call" | custom-call | flops 4429185024 | bytes 17301504 | tf_op jit(solution)/shard_map/down/pallas_call | solution.py:268
  266.2 0.0 copy-start.1
  266.2 1.2 collective-permute-start.4
  267.4 10.4 %down.9.mine_ref = bf16[256,1536]{1,0:T(8,128)(2,1)} custom-call(bf16[512,4096]{1,0:T(8,128)(2,1)} %gate_up.3.refs_0_, bf16[256,1536]{1,0:T(8,128)(2,1)} %attend.5.refs_1_, bf16[4096,3072]{1,0:T(8,128)(2,1)} %refs_2_.9, bf16[1536,3072]{1,0:T(8,128)(2,1)} %refs_3_.9), custom_call_target="tpu_custom_call" | custom-call | flops 4429185024 | bytes 17301504 | tf_op jit(solution)/shard_map/down/pallas_call | solution.py:268
  277.8 0.3 collective-permute-start.3
  278.1 0.0 copy-done.1
  278.1 1.2 collective-permute-start.7
  279.3 2.1 reshape.42
  281.4 2.1 reshape.43
  283.6 21.3 %collective-permute-done.7.other_ref = bf16[512,512]{1,0:T(8,128)(2,1)} collective-permute-done((bf16[512,512]{1,0:T(8,128)(2,1)S(1)}, bf16[512,512]{1,0:T(8,128)(2,1)}, u32[]{:S(2)}, u32[]{:S(2)}) %collective-permute-start.7) | collective-permute-done | bytes 524320 | tf_op jit(solution)/shard_map/ppermute | solution.py:357
  304.9 2.1 add.32.refs_0_
  307.0 0.0 collective-permute-done.6.other_ref
  307.0 0.0 copy-start
  307.0 1.5 copy-done
  308.5 4.8 %add.33.refs_0_ = bf16[1024,3072]{1,0:T(8,128)(2,1)} custom-call(bf16[1024,3072]{1,0:T(8,128)(2,1)} %x_ref.11, bf16[512,2560]{1,0:T(8,128)(2,1)} %down.6.mine_ref, bf16[512,2560]{1,0:T(8,128)(2,1)} %copy-done, bf16[1024,3072]{1,0:T(8,128)(2,1)} %add.32.refs_0_), custom_call_target="tpu_custom_call", output_to_operand_aliasing={{}: (3, {})} | custom-call | flops 3932160 | bytes 10485760 | tf_op jit(solution)/shard_map/add/pallas_call | solution.py:296
  313.3 0.0 collective-permute-done.5.other_ref
  313.3 4.1 %add.34.refs_0_ = bf16[1024,3072]{1,0:T(8,128)(2,1)} custom-call(bf16[1024,3072]{1,0:T(8,128)(2,1)} %x_ref.11, bf16[256,3072]{1,0:T(8,128)(2,1)} %down.7.mine_ref, bf16[256,3072]{1,0:T(8,128)(2,1)} %collective-permute-done.5.other_ref, bf16[1024,3072]{1,0:T(8,128)(2,1)} %add.33.refs_0_), custom_call_target="tpu_custom_call", output_to_operand_aliasing={{}: (3, {})} | custom-call | flops 2359296 | bytes 6291456 | tf_op jit(solution)/shard_map/add/pallas_call | solution.py:296
  317.4 0.0 collective-permute-done.4.other_ref
  317.4 2.8 add.35.refs_0_
  320.1 0.0 collective-permute-done.3.other_ref
  320.1 2.8 add.36
  (1 shorter events, 0.0 us)
Async XLA Ops:
  19.9 48.6 %collective-permute-start.1 = (bf16[4,2,1024,128]{3,2,1,0:T(8,128)(2,1)}, bf16[4,2,1024,128]{3,2,1,0:T(8,128)(2,1)S(1)}, u32[]{:S(2)}, u32[]{:S(2)}) collective-permute-start(bf16[4,2,1024,128]{3,2,1,0:T(8,128)(2,1)} %get-tuple-element.19.refs_0_), channel_id=1, source_target_pairs={{0,2},{1,3},{4,6},{5,7}} | collective-permute-start | bytes 6291464 | tf_op jit(solution)/shard_map/ppermute | solution.py:332
  21.2 83.9 %collective-permute-start = (bf16[4,2,1024,128]{3,2,1,0:T(8,128)(2,1)}, bf16[4,2,1024,128]{3,2,1,0:T(8,128)(2,1)}, u32[]{:S(2)}, u32[]{:S(2)}) collective-permute-start(bf16[4,2,1024,128]{3,2,1,0:T(8,128)(2,1)} %get-tuple-element.19.refs_0_), channel_id=1, source_target_pairs={{0,1},{2,3},{4,5},{6,7}} | collective-permute-start | bytes 6291464 | tf_op jit(solution)/shard_map/ppermute | solution.py:333
  68.5 36.1 %copy-start.2 = (bf16[4,2,1024,128]{3,2,1,0:T(8,128)(2,1)}, bf16[4,2,1024,128]{3,2,1,0:T(8,128)(2,1)S(1)}, u32[]{:S(2)}) copy-start(bf16[4,2,1024,128]{3,2,1,0:T(8,128)(2,1)S(1)} %collective-permute-done.1.refs_2_) | copy-start | bytes 6291460
  68.5 36.6 %collective-permute-start.2 = (bf16[4,2,1024,128]{3,2,1,0:T(8,128)(2,1)S(1)}, bf16[4,2,1024,128]{3,2,1,0:T(8,128)(2,1)}, u32[]{:S(2)}, u32[]{:S(2)}) collective-permute-start(bf16[4,2,1024,128]{3,2,1,0:T(8,128)(2,1)S(1)} %collective-permute-done.1.refs_2_), channel_id=1, source_target_pairs={{2,3},{3,2},{6,7},{7,6}} | collective-permute-start | bytes 6291464 | tf_op jit(solution)/shard_map/ppermute | solution.py:334
  165.2 141.8 %collective-permute-start.6 = (bf16[512,2560]{1,0:T(8,128)(2,1)}, bf16[512,2560]{1,0:T(8,128)(2,1)S(1)}, u32[]{:S(2)}, u32[]{:S(2)}) collective-permute-start(bf16[512,2560]{1,0:T(8,128)(2,1)} %down.6.mine_ref), channel_id=1, source_target_pairs={{0,4},{4,0},{1,5},{5,1},{2,6},{6,2},{3,7},{7,3}} | collective-permute-start | bytes 7864328 | tf_op jit(solution)/shard_map/ppermute | solution.py:357
  235.3 78.0 %collective-permute-start.5 = (bf16[256,3072]{1,0:T(8,128)(2,1)}, bf16[256,3072]{1,0:T(8,128)(2,1)}, u32[]{:S(2)}, u32[]{:S(2)}) collective-permute-start(bf16[256,3072]{1,0:T(8,128)(2,1)} %down.7.mine_ref), channel_id=1, source_target_pairs={{0,4},{4,0},{1,5},{5,1},{2,6},{6,2},{3,7},{7,3}} | collective-permute-start | bytes 4718600 | tf_op jit(solution)/shard_map/ppermute | solution.py:357
  266.2 11.9 %copy-start.1 = (bf16[512,512]{1,0:T(8,128)(2,1)S(1)}, bf16[512,512]{1,0:T(8,128)(2,1)}, u32[]{:S(2)}) copy-start(bf16[512,512]{1,0:T(8,128)(2,1)} %down.5.mine_ref) | copy-start | bytes 1572868
  266.2 51.1 %collective-permute-start.4 = (bf16[256,1536]{1,0:T(8,128)(2,1)}, bf16[256,1536]{1,0:T(8,128)(2,1)}, u32[]{:S(2)}, u32[]{:S(2)}) collective-permute-start(bf16[256,1536]{1,0:T(8,128)(2,1)} %down.8.mine_ref), channel_id=1, source_target_pairs={{0,4},{4,0},{1,5},{5,1},{2,6},{6,2},{3,7},{7,3}} | collective-permute-start | bytes 2359304 | tf_op jit(solution)/shard_map/ppermute | solution.py:357
  277.8 42.3 %collective-permute-start.3 = (bf16[256,1536]{1,0:T(8,128)(2,1)}, bf16[256,1536]{1,0:T(8,128)(2,1)}, u32[]{:S(2)}, u32[]{:S(2)}) collective-permute-start(bf16[256,1536]{1,0:T(8,128)(2,1)} %down.9.mine_ref), channel_id=1, source_target_pairs={{0,4},{4,0},{1,5},{5,1},{2,6},{6,2},{3,7},{7,3}} | collective-permute-start | bytes 2359304 | tf_op jit(solution)/shard_map/ppermute | solution.py:357
  278.1 26.7 %collective-permute-start.7 = (bf16[512,512]{1,0:T(8,128)(2,1)S(1)}, bf16[512,512]{1,0:T(8,128)(2,1)}, u32[]{:S(2)}, u32[]{:S(2)}) collective-permute-start(bf16[512,512]{1,0:T(8,128)(2,1)S(1)} %copy-done.1), channel_id=1, source_target_pairs={{0,4},{4,0},{1,5},{5,1},{2,6},{6,2},{3,7},{7,3}} | collective-permute-start | bytes 1572872 | tf_op jit(solution)/shard_map/ppermute | solution.py:357
  307.0 1.5 copy-start
